TPU v7x, 8 devices: a whole 2x2x1 slice. The times are simulated.
8 devices in a mesh: dp: 2 (over z, y), stage: 2 (over x), tp: 2 (over core).
Axes of the slice: x: 2, y: 2, z: 1, core: 2. Of those that a mesh axis runs over, the one named last changes fastest.
Arguments:
- act_in: bfloat16 [2, 4, 28, 28, 1024], P('stage', ('dp', 'tp'))
- w_conv: bfloat16 [2, 3, 3, 1024, 1024], P('stage', None, None, 'tp')
- w_short: bfloat16 [2, 1024, 1024], P('stage', 'tp')
- gamma: float32 [2, 1024], P('stage', 'tp')
- beta: float32 [2, 1024], P('stage', 'tp')
- gamma_s: float32 [2, 1024], P('stage', 'tp')
- grad_z: bfloat16 [2, 4, 28, 28, 1024], P('stage', 'dp', None, None, 'tp')
Outputs:
- output 1: bfloat16 [2, 4, 28, 28, 1024], P('stage', 'dp', None, None, 'tp')
- output 2: bfloat16 [2, 4, 28, 28, 1024], P('stage', ('dp', 'tp'))
- output 3: float32 [2, 3, 3, 1024, 1024], P('stage', None, None, 'tp')
- output 4: float32 [2, 1024, 1024], P('stage', 'tp')
All inputs are finite; a program needn't handle non-finite values.
Results may differ from a plain program's by a relative error of at most 0.0027.
Values are sent between devices in bfloat16 or wider.
A program may use at most 1 GiB of HBM per device.

v0:
```python
import jax
import jax.numpy as jnp
from jax import lax
from jax.sharding import PartitionSpec as P


def conv_same(left_op, right_op, right_spec):
    return lax.conv_general_dilated(left_op, right_op, (1, 1), "SAME", dimension_numbers=("NHWC", right_spec, "NHWC"), preferred_element_type=jnp.float32)


def weight_grad(images_in, grads_out):
    return lax.conv_general_dilated(images_in, grads_out, (1, 1), ((1, 1), (1, 1)), dimension_numbers=("CHWN", "IHWO", "HWNC"), preferred_element_type=jnp.float32)


def solution(mesh):
    act_spec = P("stage", ("dp", "tp"), None, None, None)
    kernel_spec = P("stage", None, None, "tp", None)
    short_spec = P("stage", "tp", None)
    vec_spec = P("stage", "tp")
    grad_spec = P("stage", "dp", None, None, "tp")

    def device_step(act_in, w_conv, w_short, gamma, beta, gamma_s, grad_z):
        by_channel = lax.all_to_all(act_in[0], "tp", 3, 0, tiled=True)
        act_local = lax.ppermute(by_channel, "stage", perm=[(0, 1)])
        kernel = w_conv[0]
        short_w = w_short[0]
        scale_main = gamma[0]
        shift_main = beta[0]
        scale_short = gamma_s[0]
        pre_part = conv_same(act_local, kernel, "HWIO")
        short_part = jnp.einsum("nhwc,co->nhwo", act_local, short_w, preferred_element_type=jnp.float32)
        pre_sum, short_sum = lax.psum_scatter((pre_part, short_part), "tp", scatter_dimension=3, tiled=True)
        mixed_sum = pre_sum * scale_main + shift_main + short_sum * scale_short
        z_val = jnp.maximum(mixed_sum, 0.0).astype(jnp.bfloat16)
        mask_pos = mixed_sum > 0.0
        grad_here = grad_z[0]
        g_main = jnp.where(mask_pos, grad_here * scale_main, 0.0).astype(jnp.bfloat16)
        g_short = jnp.where(mask_pos, grad_here * scale_short, 0.0).astype(jnp.bfloat16)
        g_main_all, g_short_all = lax.all_gather((g_main, g_short), "tp", axis=3, tiled=True)
        grad_wide = conv_same(g_main_all, kernel[::-1, ::-1], "HWOI") + jnp.einsum("nhwo,co->nhwc", g_short_all, short_w, preferred_element_type=jnp.float32)
        grad_local = grad_wide.astype(jnp.bfloat16)
        dw_part = weight_grad(act_local, g_main_all)
        dws_part = jnp.einsum("nhwc,nhwo->co", act_local, g_short_all, preferred_element_type=jnp.float32)
        dw_sum, dws_sum = lax.psum((dw_part, dws_part), "dp")
        returned = lax.ppermute(grad_local, "stage", perm=[(1, 0)])
        grad_act = lax.all_to_all(returned, "tp", 0, 3, tiled=True)
        return z_val[None], grad_act[None], dw_sum[None], dws_sum[None]

    return jax.shard_map(device_step, mesh=mesh, in_specs=(act_spec, kernel_spec, short_spec, vec_spec, vec_spec, vec_spec, grad_spec), out_specs=(grad_spec, act_spec, kernel_spec, short_spec), check_vma=False)
```

profile of v0, /device:TPU:2, one launch (start us, length us, event | category | flops | bytes accessed | tf_op | source)
XLA Modules:
  0.0 767.7 jit_solution(9096875926234464529)
XLA Ops:
  7.2 0.0 copy-start
  7.2 0.0 reduce-scatter.3.cloned.1.call-start
  7.2 14.6 %copy.54 = bf16[1,1,28,28,1024]{3,2,4,1,0:T(8,128)(2,1)} copy(bf16[1,1,28,28,1024]{4,3,2,1,0:T(8,128)(2,1)} %param.7) | data formatting | bytes 3211264 | tf_op args[0]
  21.8 8.2 %bitcast_bitcast_fusion = bf16[1024,1,28,28]{3,2,1,0:T(8,128)(2,1)} fusion(bf16[1,1,28,28,1024]{3,2,4,1,0:T(8,128)(2,1)} %copy.54), kind=kLoop, calls=%fused_computation.46 | loop fusion | bytes 3211264
  30.0 11.9 %reshape.37 = bf16[2,2,200704]{2,1,0:T(2,128)(2,1)S(1)} reshape(bf16[1024,1,28,28]{3,2,1,0:T(8,128)(2,1)} %bitcast_bitcast_fusion) | data formatting | bytes 3211264
  42.0 6.2 all_to_all.33
  48.2 11.9 %reshape.38 = bf16[1024,1,28,28]{3,2,1,0:T(8,128)(2,1)} reshape(bf16[2,2,200704]{2,1,0:T(2,128)(2,1)} %all_to_all.33) | data formatting | bytes 3211264
  60.1 15.1 %copy.75 = bf16[1,28,28,2,512]{4,3,2,1,0:T(2,128)(2,1)S(1)} copy(bf16[1,28,28,2,512]{2,1,4,3,0:T(8,128)(2,1)} %bitcast.74) | data formatting | bytes 3211264 | tf_op jit(solution)/shard_map/all_to_all | solution.py:23
  75.2 1.3 collective-permute-start
  76.5 37.8 %collective-permute-done = bf16[2,28,28,512]{3,0,2,1:T(2,128)(2,1)S(1)} collective-permute-done((bf16[2,28,28,512]{3,0,2,1:T(2,128)(2,1)S(1)}, bf16[2,28,28,512]{3,0,2,1:T(2,128)(2,1)S(1)}, u32[]{:S(2)}, u32[]{:S(2)}) %collective-permute-start) | collective-permute-done | bytes 1605664 | tf_op jit(solution)/shard_map/ppermute | solution.py:24
  114.3 1.9 pad
  116.2 1.1 copy.57
  117.4 0.2 slice.4
  117.6 0.0 copy-done.3
  117.6 0.0 copy-done.9
  117.6 27.0 %broadcast_select_fusion = f32[28,16,4,1024]{3,1,2,0:T(8,128)S(1)} fusion(pred[16,4]{0,1:T(4,128)(4,1)S(1)} %copy-done.9, bf16[1,3,3,512,1024]{4,3,2,1,0:T(8,128)(2,1)} %param.8, bf16[28,2,7,2,512]{4,2,1,3,0:T(8,128)(2,1)S(1)} %slice.4, bf16[28,2,8,4,512]{4,2,1,3,0:T(8,128)(2,1)S(1)} %copy.57), kind=kOutput, calls=%fused_computation.24 | convolution fusion | flops 16518873088 | bytes 19415104 | tf_op jit(solution)/shard_map/conv_general_dilated | solution.py:8
  144.7 9.2 %copy.58 = f32[28,16,4,1024]{3,2,1,0:T(4,128)} copy(f32[28,16,4,1024]{3,1,2,0:T(8,128)S(1)} %broadcast_select_fusion) | data formatting | bytes 14680064 | tf_op jit(solution)/shard_map/conv_general_dilated | solution.py:8
  153.8 10.0 %reshape.20 = f32[28,2,32,1024]{3,2,1,0:T(8,128)} reshape(f32[28,16,4,1024]{3,2,1,0:T(4,128)} %copy.58) | data formatting | bytes 14680064 | tf_op jit(solution)/shard_map/conv_general_dilated | solution.py:8
  163.8 7.4 copy_bitcast_fusion
  171.3 0.0 reduce-scatter.3.cloned.1.call-update
  171.3 0.0 reduce-scatter.5.cloned.1.call-start
  171.3 0.0 copy-done
  171.3 1.3 copy-done.4
  172.7 5.1 fusion.33
  177.8 0.0 reduce-scatter.5.cloned.1.call-update
  177.8 0.0 all-gather.5.cloned.1.call-start
  177.9 5.8 reduce-scatter.3.cloned.1.call-done
  183.6 15.0 %reduce-scatter.5.cloned.1.call-done = f32[2,28,28,512]{3,2,1,0:T(8,128)} async-done(((f32[2,28,28,1024]{3,2,1,0:T(8,128)}), f32[2,28,28,512]{3,2,1,0:T(8,128)}) %reduce-scatter.5.cloned.1.call-update) | async-done | bytes 3211280 | tf_op jit(solution)/shard_map/reduce_scatter | solution.py:32
  198.7 0.0 copy-done.2
  198.7 0.0 copy-done.6
  198.7 0.0 copy-done.8
  198.7 5.3 fusion.12
  204.0 0.0 all-gather.5.cloned.1.call-update
  204.0 0.0 all-gather.3.cloned.1.call-start
  204.0 3.2 fusion.10
  207.3 0.0 all-gather.3.cloned.1.call-update
  207.3 0.0 copy-start.5
  207.3 0.0 all-reduce.3.cloned.1.call-start
  207.4 8.3 %all-gather.5.cloned.1.call-done = bf16[2,28,28,1024]{3,2,1,0:T(8,128)(2,1)} async-done(((bf16[2,28,28,512]{3,2,1,0:T(8,128)(2,1)}), bf16[2,28,28,1024]{3,2,1,0:T(8,128)(2,1)}) %all-gather.5.cloned.1.call-update) | async-done | bytes 3211280 | tf_op jit(solution)/shard_map/all_gather | solution.py:39
  215.7 5.9 fusion.35
  221.6 7.6 all-gather.3.cloned.1.call-done
  229.2 50.5 %convolution_bitcast_fusion = f32[1,3,3,512,1024]{4,3,2,1,0:T(8,128)} fusion(bf16[2,28,28,512]{3,0,2,1:T(2,128)(2,1)S(1)} %copy-done.5, bf16[2,28,28,1024]{3,2,1,0:T(8,128)(2,1)} %all-gather.3.cloned.1.call-done), kind=kOutput, calls=%fused_computation.6 | convolution fusion | flops 14101250048 | bytes 23691264 | tf_op jit(solution)/shard_map/conv_general_dilated | solution.py:12
  279.7 0.0 all-reduce.3.cloned.1.call-update
  279.8 6.2 pad.2
  286.0 6.6 reshape.23
  292.6 3.0 slice.6
  295.6 0.0 copy-start.10
  295.6 5.3 fusion.5
  301.0 30.8 %fusion.26 = f32[28,16,4,512]{3,1,2,0:T(8,128)S(1)} fusion(bf16[1,3,3,512,1024]{4,3,2,1,0:T(8,128)(2,1)} %param.8, bf16[28,2,8,6,1024]{4,3,2,0,1:T(8,128)(2,1)S(1)} %fusion.5, pred[16,4]{0,1:T(4,128)(4,1)S(1)} %copy-done.10), kind=kOutput, calls=%fused_computation.33 | convolution fusion | flops 16509698048 | bytes 18612288 | tf_op jit(solution)/shard_map/conv_general_dilated | solution.py:8
  331.8 5.0 copy.63
  336.7 5.2 reshape.27
  341.9 5.3 fusion.14
  347.2 0.0 copy-start.1
  347.2 1.7 copy.65
  348.9 2.3 collective-permute-start.1
  351.2 2.8 copy.71
  354.0 31.8 %collective-permute-done.1 = bf16[2,28,28,512]{3,0,2,1:T(2,128)(2,1)S(1)} collective-permute-done((bf16[2,28,28,512]{3,0,2,1:T(2,128)(2,1)S(1)}, bf16[2,28,28,512]{3,0,2,1:T(2,128)(2,1)S(1)}, u32[]{:S(2)}, u32[]{:S(2)}) %collective-permute-start.1) | collective-permute-done | bytes 1605664 | tf_op jit(solution)/shard_map/ppermute | solution.py:45
  385.8 0.4 copy.66
  386.2 5.5 all_to_all.34
  391.6 1.7 copy.67
  393.3 1.9 broadcast_in_dim.16
  395.2 347.7 %all-reduce.3.cloned.1.call-done = (f32[1,3,3,512,1024]{4,3,2,1,0:T(8,128)}, f32[1,512,1024]{1,2,0:T(8,128)}) async-done(((f32[1,3,3,512,1024]{4,3,2,1,0:T(8,128)}, f32[1,512,1024]{1,2,0:T(8,128)}), (f32[1,3,3,512,1024]{4,3,2,1,0:T(8,128)}, f32[1,512,1024]{1,2,0:T(8,128)})) %all-reduce.3.cloned.1.call-update) | async-done | bytes 20971536 | tf_op jit(solution)/shard_map/psum | solution.py:44
  742.9 2.9 copy.72
  745.8 15.1 %copy.106 = f32[1,3,3,512,1024]{4,3,2,1,0:T(8,128)} copy(f32[1,3,3,512,1024]{4,3,2,1,0:T(8,128)} %get-tuple-element.27) | data formatting | bytes 37748736
  (11 shorter events, 0.0 us)
Async XLA Ops:
  7.2 164.2 %copy-start = (bf16[1,512,1024]{2,1,0:T(8,128)(2,1)S(1)}, bf16[1,512,1024]{2,1,0:T(8,128)(2,1)}, u32[]{:S(2)}) copy-start(bf16[1,512,1024]{2,1,0:T(8,128)(2,1)} %param.9) | copy-start | bytes 3145732
  7.2 176.5 %reduce-scatter.3.cloned.1.call-start = ((), (), s32[]{:S(2)}) async-start(), calls=%async_computation.4 | async-start | bytes 11010048 | tf_op jit(solution)/shard_map/reduce_scatter | solution.py:32
  75.2 39.1 %collective-permute-start = (bf16[2,28,28,512]{3,0,2,1:T(2,128)(2,1)S(1)}, bf16[2,28,28,512]{3,0,2,1:T(2,128)(2,1)S(1)}, u32[]{:S(2)}, u32[]{:S(2)}) collective-permute-start(bf16[2,28,28,512]{3,0,2,1:T(2,128)(2,1)S(1)} %bitcast.78), channel_id=1, source_target_pairs={{0,2},{1,3},{4,6},{5,7}} | collective-permute-start | bytes 4816904 | tf_op jit(solution)/shard_map/ppermute | solution.py:24
  114.3 3.3 copy-start.3
  114.3 3.3 copy-start.9
  171.3 1.4 copy-start.4
  171.3 27.4 %reduce-scatter.5.cloned.1.call-start = ((), (), s32[]{:S(2)}) async-start(), calls=%async_computation.5 | async-start | bytes 11010048 | tf_op jit(solution)/shard_map/reduce_scatter | solution.py:32
  177.8 20.9 %copy-start.2 = (bf16[1,2,28,28,512]{4,1,3,2,0:T(2,128)(2,1)S(1)}, bf16[1,2,28,28,512]{4,1,3,2,0:T(2,128)(2,1)}, u32[]{:S(2)}) copy-start(bf16[1,2,28,28,512]{4,1,3,2,0:T(2,128)(2,1)} %param.13) | copy-start | bytes 4816900
  177.8 20.9 %copy-start.6 = (f32[1,512]{1,0:T(1,128)S(1)}, f32[1,512]{1,0:T(1,128)}, u32[]{:S(2)}) copy-start(f32[1,512]{1,0:T(1,128)} %param.10) | copy-start | bytes 6148
  177.8 20.9 %copy-start.7 = (f32[1,512]{1,0:T(1,128)S(1)}, f32[1,512]{1,0:T(1,128)}, u32[]{:S(2)}) copy-start(f32[1,512]{1,0:T(1,128)} %param.12) | copy-start | bytes 6148
  177.8 20.9 %copy-start.8 = (f32[1,512]{1,0:T(1,128)S(1)}, f32[1,512]{1,0:T(1,128)}, u32[]{:S(2)}) copy-start(f32[1,512]{1,0:T(1,128)} %param.11) | copy-start | bytes 6148
  177.8 37.9 %all-gather.5.cloned.1.call-start = ((), (), s32[]{:S(2)}) async-start(), calls=%async_computation.7 | async-start | bytes 5505024 | tf_op jit(solution)/shard_map/all_gather | solution.py:39
  204.0 25.2 %all-gather.3.cloned.1.call-start = ((), (), s32[]{:S(2)}) async-start(), calls=%async_computation.6 | async-start | bytes 5505024 | tf_op jit(solution)/shard_map/all_gather | solution.py:39
  207.3 21.9 %copy-start.5 = (bf16[2,28,28,512]{3,0,2,1:T(2,128)(2,1)S(1)}, bf16[2,28,28,512]{3,0,2,1:T(2,128)(2,1)}, u32[]{:S(2)}) copy-start(bf16[2,28,28,512]{3,0,2,1:T(2,128)(2,1)} %copy-done.3) | copy-start | bytes 4816900
  207.3 535.6 %all-reduce.3.cloned.1.call-start = ((), (), s32[]{:S(2)}) async-start(), calls=%async_computation.8 | async-start | bytes 41943040 | tf_op jit(solution)/shard_map/psum | solution.py:44
  295.6 5.3 copy-start.10
  347.2 4.0 copy-start.1
  348.9 36.9 %collective-permute-start.1 = (bf16[2,28,28,512]{3,0,2,1:T(2,128)(2,1)S(1)}, bf16[2,28,28,512]{3,0,2,1:T(2,128)(2,1)S(1)}, u32[]{:S(2)}, u32[]{:S(2)}) collective-permute-start(bf16[2,28,28,512]{3,0,2,1:T(2,128)(2,1)S(1)} %copy.65), channel_id=1, source_target_pairs={{2,0},{3,1},{6,4},{7,5}} | collective-permute-start | bytes 4816904 | tf_op jit(solution)/shard_map/ppermute | solution.py:45
Sparse Core Ops, SparseCore 0:
  171.4 12.2 reduce-scatter.2
  186.5 12.1 reduce-scatter.4
  204.1 11.5 all-gather.4
  217.6 11.5 all-gather.2
  279.9 462.9 all-reduce.2
where the time goes:
time: 777 us; the launch traced here: 768 us
  waiting for transfers between devices  454 us (58%)
  local copies, waits for them, and re-layouts  145 us (19%)
  matrix products  125 us (16%)
  between operations  14.3 us (2%)
  other arithmetic  13.8 us (2%)
  blocking collectives  11.7 us (2%)
    psum x1, waiting for transfers between devices, device_step(): dw_sum, dws_sum = lax.psum((dw_part, dws_part), 'dp')  348 us
    unnamed x29, local copies, waits for them, and re-layouts  68.8 us
    conv_general_dilated x2, matrix products, conv_same(): lax.conv_general_dilated(left_op, right_op, (1, 1), 'SAME', dimension_num...  57.9 us
    conv_general_dilated x1, matrix products, weight_grad(): lax.conv_general_dilated(images_in, grads_out, (1, 1), ((1, 1), (1, 1)),...  50.5 us
    conv_general_dilated x9, local copies, waits for them, and re-layouts, conv_same(): lax.conv_general_dilated(left_op, right_op, (1, 1), 'SAME', dimension_num...  47.7 us
    ppermute x1, waiting for transfers between devices, device_step(): act_local = lax.ppermute(by_channel, 'stage', perm=[(0, 1)])  37.8 us
    ppermute x1, waiting for transfers between devices, device_step(): returned = lax.ppermute(grad_local, 'stage', perm=[(1, 0)])  31.8 us
    reduce_scatter x2, waiting for transfers between devices, device_step(): lax.psum_scatter((pre_part, short_part), 'tp', scatter_dimension=3, tiled...  20.8 us
  transfers between devices with their start and end apart: 7, of which 7 were waited for; matrix products, arithmetic and copies ran while one was open for 12% of the time, Pallas kernels for 0%

commit v1 on v0

v1 whole, which is shorter than its diff:
```python
import functools

import jax
import jax.numpy as jnp
from jax import lax
from jax.experimental import pallas as pl
from jax.experimental.pallas import tpu as pltpu
from jax.sharding import PartitionSpec as P


SIDE = 28
LO = 7
GRP = 16
HAL = LO + 2
GROUPS = HAL * HAL + LO * LO
PIX = SIDE * SIDE
HALF = 512
CH = 1024
TILE = 256
F32 = jnp.float32
BF16 = jnp.bfloat16
VMEM_LIMIT = 60 * 1024 * 1024


def params(n_axes):
    return pltpu.CompilerParams(dimension_semantics=("arbitrary",) * n_axes, vmem_limit_bytes=VMEM_LIMIT)


def cost(flops, bytes_accessed):
    return pl.CostEstimate(flops=int(flops), bytes_accessed=int(bytes_accessed), transcendentals=0)


def order_matrix(transposed):
    shape = (128, 112) if transposed else (112, 128)
    row = lax.broadcasted_iota(jnp.int32, shape, 1 if transposed else 0)
    col = lax.broadcasted_iota(jnp.int32, shape, 0 if transposed else 1)
    w_lo, h_hi, w_hi = row // 16, (row // 4) % 4, row % 4
    return (col == h_hi * 32 + w_hi * 7 + w_lo).astype(F32).astype(BF16)


def to_blocks_kernel(t_ref, img_ref, own_ref, peer_ref, *rest):
    pad_ref = rest[-1]
    pad_ref[...] = jnp.zeros_like(pad_ref)
    pad_ref[:, :SIDE, :] = img_ref[...]
    select = order_matrix(False)
    step = pl.program_id(0)
    for lo in range(LO):
        rows = jnp.concatenate([pad_ref[hi * LO + lo] for hi in range(4)], axis=0)
        out = jnp.dot(select, rows, preferred_element_type=F32).astype(BF16)
        part = slice(lo * 112, (lo + 1) * 112)

        @pl.when(step == 0)
        def _():
            own_ref[part, :] = out

        @pl.when(step == 1)
        def _():
            peer_ref[part, :] = out

        if len(rest) > 1:
            rest[0][part, :] = out


def to_blocks(me, array, in_map, joined):
    plane = pl.BlockSpec((PIX, HALF), lambda k, t: (0, 0))
    return pl.pallas_call(
        to_blocks_kernel,
        grid_spec=pltpu.PrefetchScalarGridSpec(
            num_scalar_prefetch=1,
            grid=(2,),
            in_specs=[pl.BlockSpec((None, None, SIDE, SIDE, HALF), in_map)],
            out_specs=[plane, plane] + ([pl.BlockSpec((PIX, HALF), lambda k, t: (0, k))] if joined else []),
            scratch_shapes=[pltpu.VMEM((SIDE, 32, HALF), BF16)],
        ),
        out_shape=[jax.ShapeDtypeStruct((PIX, HALF), BF16)] * 2
        + ([jax.ShapeDtypeStruct((PIX, CH), BF16)] if joined else []),
        compiler_params=params(1),
        cost_estimate=cost(2 * 2 * 7 * 112 * 128 * HALF * 2, 2 * 2 * PIX * HALF * 2),
        name="to_blocks",
    )(me, array)


def from_blocks_kernel(idx_ref, z_ref, z_near_ref, dx_own_ref, dx_peer_ref, z_out, dx_out):
    select = order_matrix(True)
    step = pl.program_id(0)
    stage = idx_ref[1]

    def emit(ref, out_ref):
        for lo in range(LO):
            rows = jnp.dot(select, ref[lo * 112:(lo + 1) * 112, :], preferred_element_type=F32).astype(BF16)
            for hi in range(4):
                out_ref[hi * LO + lo] = rows[hi * 32:hi * 32 + SIDE, :]

    @pl.when(stage == 0)
    def _():
        z_out[...] = jnp.zeros_like(z_out)

        @pl.when(step == 0)
        def _():
            emit(dx_own_ref, dx_out)

        @pl.when(step == 1)
        def _():
            emit(dx_peer_ref, dx_out)

    @pl.when(stage == 1)
    def _():
        dx_out[...] = jnp.zeros_like(dx_out)

        @pl.when(step == 0)
        def _():
            emit(z_ref, z_out)

        @pl.when(step == 1)
        def _():
            emit(z_near_ref, z_out)


def from_blocks(idx, z, z_near, dx_own, dx_peer):
    return pl.pallas_call(
        from_blocks_kernel,
        grid_spec=pltpu.PrefetchScalarGridSpec(
            num_scalar_prefetch=1,
            grid=(2,),
            in_specs=[
                pl.BlockSpec((PIX, HALF), lambda k, m: (0, 0)),
                pl.BlockSpec((PIX, HALF), lambda k, m: (0, 1)),
                pl.BlockSpec((PIX, HALF), lambda k, m: (0, 0)),
                pl.BlockSpec((PIX, HALF), lambda k, m: (0, 0)),
            ],
            out_specs=[
                pl.BlockSpec((None, None, SIDE, SIDE, HALF), lambda k, m: (0, (m[0] + k) % 2, 0, 0, 0)),
                pl.BlockSpec((None, None, SIDE, SIDE, HALF), lambda k, m: (0, 0, 0, 0, (m[0] + k) % 2)),
            ],
        ),
        out_shape=[
            jax.ShapeDtypeStruct((1, 2, SIDE, SIDE, HALF), BF16),
            jax.ShapeDtypeStruct((1, 1, SIDE, SIDE, CH), BF16),
        ],
        compiler_params=params(1),
        cost_estimate=cost(2 * 2 * 7 * 112 * 128 * HALF * 2, 4 * 2 * PIX * HALF * 2),
        name="from_blocks",
    )(idx, z, z_near, dx_own, dx_peer)


def moved(tile, step_h, step_w):
    wide = tile.astype(F32)
    n = wide.shape[1]
    if step_h < 0:
        wide = jnp.concatenate([jnp.zeros((4, n), F32), wide[:12]], axis=0)
    if step_h > 0:
        wide = jnp.concatenate([wide[4:], jnp.zeros((4, n), F32)], axis=0)
    if step_w:
        w_hi = lax.broadcasted_iota(jnp.int32, (GRP, n), 0) % 4
        if step_w < 0:
            wide = jnp.concatenate([wide[15:], wide[:15]], axis=0)
            wide = jnp.where(w_hi == 0, 0.0, wide)
        else:
            wide = jnp.concatenate([wide[1:], wide[:1]], axis=0)
            wide = jnp.where(w_hi == 3, 0.0, wide)
    return wide.astype(BF16)


def fill_halo(dst_ref, value):
    n = value.shape[1]
    groups = value.reshape(LO, LO, GRP, n)
    for a in range(HAL):
        step_h = -1 if a == 0 else (1 if a == HAL - 1 else 0)
        if not step_h:
            dst_ref[a * HAL + 1:a * HAL + 1 + LO] = groups[a - 1]
        for b in range(HAL):
            step_w = -1 if b == 0 else (1 if b == HAL - 1 else 0)
            if step_h or step_w:
                dst_ref[a * HAL + b] = moved(groups[(a - 1) % LO, (b - 1) % LO], step_h, step_w)


def window(ref, i, j):
    parts = [ref[pl.ds((i + a) * HAL + j, LO)] for a in range(LO)]
    whole = jnp.concatenate(parts, axis=0)
    return whole.reshape(PIX, whole.shape[-1])


def forward_sums(xh_ref, w_ref, s_ref, pre, short):
    for i in range(3):
        for j in range(3):
            term = jnp.dot(window(xh_ref, i, j), w_ref[i * 3 + j], preferred_element_type=F32)
            pre = term if pre is None else pre + term
    term = jnp.dot(window(xh_ref, 1, 1), s_ref[...], preferred_element_type=F32)
    return pre, term if short is None else short + term


def fwd_first_kernel(x_ref, w_ref, s_ref, pre_ref, short_ref, xh_ref):
    @pl.when(pl.program_id(0) == 0)
    def _():
        fill_halo(xh_ref, x_ref[...])

    pre_ref[...], short_ref[...] = forward_sums(xh_ref, w_ref, s_ref, None, None)


def fwd_last_kernel(t_ref, x_ref, w_ref, s_ref, pre_ref, short_ref, vec_ref, dza_ref, dzb_ref, z_ref, dzm_ref, g_ref, xh_ref):
    @pl.when(pl.program_id(0) == 0)
    def _():
        fill_halo(xh_ref, x_ref[...])

    pre, short = forward_sums(xh_ref, w_ref, s_ref, pre_ref[...], short_ref[...])
    u = pre * vec_ref[0:1, :] + vec_ref[1:2, :] + short * vec_ref[2:3, :]
    z_ref[...] = jnp.maximum(u, 0.0).astype(BF16)
    mine = pl.program_id(0) // 2 == t_ref[0]
    dz = jnp.where(mine, dza_ref[...].astype(F32), dzb_ref[...].astype(F32))
    dz = jnp.where(u > 0.0, dz, 0.0)
    dzm_ref[...] = dz.astype(BF16)
    both_grads(dz, vec_ref, g_ref)


def both_grads(dz, vec_ref, g_ref):
    g_ref[HAL * HAL:] = (dz * vec_ref[2:3, :]).astype(BF16).reshape(LO * LO, GRP, -1)
    fill_halo(g_ref, (dz * vec_ref[0:1, :]).astype(BF16))


FWD_FLOPS = 2 * PIX * HALF * CH * 10
W_BYTES = 10 * HALF * CH * 2


def fwd_first(x, w, s):
    return pl.pallas_call(
        fwd_first_kernel,
        grid=(CH // TILE,),
        in_specs=[
            pl.BlockSpec((PIX, HALF), lambda j: (0, 0)),
            pl.BlockSpec((9, HALF, TILE), lambda j: (0, 0, j)),
            pl.BlockSpec((HALF, TILE), lambda j: (0, j)),
        ],
        out_specs=[pl.BlockSpec((PIX, TILE), lambda j: (0, j))] * 2,
        out_shape=[jax.ShapeDtypeStruct((PIX, CH), F32)] * 2,
        scratch_shapes=[pltpu.VMEM((HAL * HAL, GRP, HALF), BF16)],
        compiler_params=params(1),
        cost_estimate=cost(FWD_FLOPS, W_BYTES),
        name="fwd_first",
    )(x, w, s)


def fwd_last(me, x, w, s, pre, short, vec, dz_own, dz_peer):
    tile = pl.BlockSpec((PIX, TILE), lambda j, t: (0, j))
    return pl.pallas_call(
        fwd_last_kernel,
        grid_spec=pltpu.PrefetchScalarGridSpec(
            num_scalar_prefetch=1,
            grid=(CH // TILE,),
            in_specs=[
                pl.BlockSpec((PIX, HALF), lambda j, t: (0, 0)),
                pl.BlockSpec((9, HALF, TILE), lambda j, t: (0, 0, j)),
                pl.BlockSpec((HALF, TILE), lambda j, t: (0, j)),
                tile,
                tile,
                pl.BlockSpec((3, TILE), lambda j, t: (0, j)),
                pl.BlockSpec((PIX, TILE), lambda j, t: (0, jnp.where(j // 2 == t[0], j % 2, 1 - t[0]))),
                pl.BlockSpec((PIX, TILE), lambda j, t: (0, jnp.where(j // 2 == t[0], t[0], j % 2))),
            ],
            out_specs=[
                pl.BlockSpec((PIX, TILE), lambda j, t: (0, (j + 2 * t[0]) % 4)),
                tile,
                pl.BlockSpec((GROUPS, GRP, TILE), lambda j, t: (0, 0, j)),
            ],
            scratch_shapes=[pltpu.VMEM((HAL * HAL, GRP, HALF), BF16)],
        ),
        out_shape=[
            jax.ShapeDtypeStruct((PIX, CH), BF16),
            jax.ShapeDtypeStruct((PIX, CH), BF16),
            jax.ShapeDtypeStruct((GROUPS, GRP, CH), BF16),
        ],
        compiler_params=params(1),
        cost_estimate=cost(FWD_FLOPS, W_BYTES),
        name="fwd_last",
    )(me, x, w, s, pre, short, vec, dz_own, dz_peer)


def grads_kernel(dzm_ref, vec_ref, g_ref):
    both_grads(dzm_ref[...].astype(F32), vec_ref, g_ref)


def grads(dzm, vec):
    return pl.pallas_call(
        grads_kernel,
        grid=(CH // TILE,),
        in_specs=[pl.BlockSpec((PIX, TILE), lambda j: (0, j)), pl.BlockSpec((3, TILE), lambda j: (0, j))],
        out_specs=pl.BlockSpec((GROUPS, GRP, TILE), lambda j: (0, 0, j)),
        out_shape=jax.ShapeDtypeStruct((GROUPS, GRP, CH), BF16),
        compiler_params=params(1),
        cost_estimate=cost(8 * PIX * CH, 8 * PIX * CH),
        name="grads",
    )(dzm, vec)


def dot_nt(a, b):
    return lax.dot_general(a, b, (((1,), (1,)), ((), ())), preferred_element_type=F32)


def dx_kernel(gh_ref, w_ref, s_ref, dx_ref):
    total = dot_nt(gh_ref[HAL * HAL:].reshape(PIX, CH), s_ref[...])
    for i in range(3):
        for j in range(3):
            total = total + dot_nt(window(gh_ref, 2 - i, 2 - j), w_ref[i * 3 + j])
    dx_ref[...] = total.astype(BF16)


def dx_half(g, w, s):
    return pl.pallas_call(
        dx_kernel,
        grid=(HALF // TILE,),
        in_specs=[
            pl.BlockSpec((GROUPS, GRP, CH), lambda j: (0, 0, 0)),
            pl.BlockSpec((9, TILE, CH), lambda j: (0, j, 0)),
            pl.BlockSpec((TILE, CH), lambda j: (j, 0)),
        ],
        out_specs=pl.BlockSpec((PIX, TILE), lambda j: (0, j)),
        out_shape=jax.ShapeDtypeStruct((PIX, HALF), BF16),
        compiler_params=params(1),
        cost_estimate=cost(FWD_FLOPS, W_BYTES),
        name="dx_half",
    )(g, w, s)


MAIN = 768


def dw_kernel(first, *refs):
    if first:
        xa_ref, xb_ref, ga_ref, gb_ref, dw_ref, ds_ref, xt_ref = refs
    else:
        xa_ref, xb_ref, ga_ref, gb_ref = refs[:4]
        x_tails, g_tails = refs[4:6], (refs[6:10], refs[10:14])
        dw_in, ds_in, dw_ref, ds_ref, xt_ref = refs[14:]
    step = pl.program_id(0)

    @pl.when(step == 0)
    def _():
        xt_ref[:, :MAIN] = xa_ref[:MAIN, :].T
        xt_ref[:, MAIN:2 * MAIN] = xb_ref[:MAIN, :].T
        if not first:
            ends = [xa_ref[MAIN:, :], xb_ref[MAIN:, :]] + [ref[...] for ref in x_tails]
            xt_ref[:, 2 * MAIN:] = jnp.concatenate(ends, axis=0).T

    def product(a, b, tails):
        parts = [a[:MAIN], b[:MAIN]]
        if not first:
            parts += [a[MAIN:], b[MAIN:]] + tails
        return jnp.dot(xt_ref[...], jnp.concatenate(parts, axis=0), preferred_element_type=F32)

    @pl.when(step < 9)
    def _():
        i, j = 2 - step // 3, 2 - step % 3
        tails = []
        if not first:
            for rows in g_tails:
                tail = rows[0][j]
                tail = jnp.where(i == 1, rows[1][j], tail)
                tails.append(jnp.where(i == 2, rows[2][j], tail))
        total = product(window(ga_ref, i, j), window(gb_ref, i, j), tails)
        dw_ref[...] = total if first else total + dw_in[...]

    @pl.when(step == 9)
    def _():
        tails = [] if first else [rows[3][0] for rows in g_tails]
        total = product(ga_ref[HAL * HAL:].reshape(PIX, -1), gb_ref[HAL * HAL:].reshape(PIX, -1), tails)
        ds_ref[...] = total if first else total + ds_in[...]


def weight_sums(xa, xb, b_col, ga, gb, tails=None, partial=None):
    first = partial is None
    g_spec = pl.BlockSpec((GROUPS, GRP, CH), lambda s: (0, 0, 0))
    dw_spec = pl.BlockSpec((None, None, None, HALF, CH), lambda s: (0, jnp.minimum(s, 8) // 3, jnp.minimum(s, 8) % 3, 0, 0))
    ds_spec = pl.BlockSpec((None, HALF, CH), lambda s: (0, 0, 0))
    x_rows = MAIN if first else PIX
    in_specs = [pl.BlockSpec((x_rows, HALF), lambda s: (0, 0)), pl.BlockSpec((x_rows, HALF), lambda s: (0, b_col)), g_spec, g_spec]
    args = [xa, xb, ga, gb]
    if not first:
        x_own, x_near, g_own, g_near = tails
        in_specs += [pl.BlockSpec((GRP, HALF), lambda s: (MAIN // GRP, 0))] * 2
        args += [x_own, x_near]
        for g in (g_own, g_near):
            for row in range(3):
                in_specs.append(pl.BlockSpec((3, GRP, CH), lambda s, row=row: (20 + 3 * row, 0, 0)))
            in_specs.append(pl.BlockSpec((1, GRP, CH), lambda s: (GROUPS - 1, 0, 0)))
            args += [g] * 4
        in_specs += [dw_spec, ds_spec]
        args += list(partial)
    return pl.pallas_call(
        functools.partial(dw_kernel, first),
        grid=(10,),
        in_specs=in_specs,
        out_specs=[dw_spec, ds_spec],
        out_shape=[jax.ShapeDtypeStruct((1, 3, 3, HALF, CH), F32), jax.ShapeDtypeStruct((1, HALF, CH), F32)],
        scratch_shapes=[pltpu.VMEM((HALF, 2 * MAIN if first else 2 * PIX + 2 * GRP), BF16)],
        input_output_aliases={} if first else {14: 0, 15: 1},
        compiler_params=params(1),
        cost_estimate=cost(2 * FWD_FLOPS, 2 * W_BYTES),
        name="weight_sums",
    )(*args)


def solution(mesh):
    act_spec = P("stage", ("dp", "tp"), None, None, None)
    kernel_spec = P("stage", None, None, "tp", None)
    short_spec = P("stage", "tp", None)
    vec_spec = P("stage", "tp")
    grad_spec = P("stage", "dp", None, None, "tp")
    swap = [(0, 1), (1, 0)]

    def block(act_in, w_conv, w_short, gamma, beta, gamma_s, grad_z):
        t = lax.axis_index("tp")
        me = t.astype(jnp.int32).reshape(1)
        idx = jnp.stack([t, lax.axis_index("stage")]).astype(jnp.int32)
        w_own = w_conv.reshape(9, HALF, CH)
        s_own = w_short.reshape(HALF, CH)

        img_own, img_peer, img = to_blocks(me, act_in, lambda k, m: (0, 0, 0, 0, (m[0] + k) % 2), True)
        x_own = lax.ppermute(img_own, "stage", [(0, 1)])
        x_peer = lax.ppermute(img_peer, "stage", [(0, 1)])
        w_peer = lax.ppermute(w_own, "tp", swap)
        s_peer = lax.ppermute(s_own, "tp", swap)
        vec_own = jnp.concatenate([gamma, beta, gamma_s], axis=0)
        vec_peer = lax.ppermute(vec_own, "tp", swap)
        vec = jnp.where(t == 0, jnp.concatenate([vec_own, vec_peer], axis=1), jnp.concatenate([vec_peer, vec_own], axis=1))
        dz_own, dz_send = to_blocks(me, grad_z, lambda k, m: (0, (m[0] + k) % 2, 0, 0, 0), False)
        dz_peer = lax.ppermute(dz_send, "tp", swap)

        far = lax.ppermute(img, "dp", swap)
        x_far = lax.ppermute(far, "stage", [(0, 1)])

        pre, short = fwd_first(x_own, w_own, s_own)
        x_near = lax.ppermute(x_peer, "tp", swap)
        z, dzm, g = fwd_last(me, x_peer, w_peer, s_peer, pre, short, vec, dz_own, dz_peer)
        dzm_far = lax.ppermute(dzm, "dp", swap)
        g_near = lax.ppermute(g, "tp", swap)
        z_near = lax.ppermute(z, "tp", swap)
        dx_own = lax.ppermute(dx_half(g, w_own, s_own), "stage", [(1, 0)])
        dx_peer = lax.ppermute(dx_half(g, w_peer, s_peer), "stage", [(1, 0)])
        x_diag = lax.ppermute(x_far, "tp", swap)
        g_far = grads(dzm_far, vec)
        g_diag = lax.ppermute(g_far, "tp", swap)

        partial = weight_sums(x_own, x_near, 0, g, g_near)
        z_out, grad_act = from_blocks(idx, z, z_near, dx_own, dx_peer)
        dw, ds = weight_sums(x_far, x_diag, 1, g_far, g_diag, (x_own, x_near, g, g_near), partial)
        return z_out, grad_act, dw, ds

    return jax.shard_map(block, mesh=mesh, in_specs=(act_spec, kernel_spec, short_spec, vec_spec, vec_spec, vec_spec, grad_spec), out_specs=(grad_spec, act_spec, kernel_spec, short_spec), check_vma=False)
```

time: 777 us -> 258 us (0.33)
  waiting for transfers between devices: 454 us -> 96.8 us
  local copies, waits for them, and re-layouts: 145 us -> 10.4 us
  Pallas kernels: 0 us -> 129 us
  matrix products: 125 us -> 0 us
  between operations: 14.3 us -> 0.76 us
  other arithmetic: 13.8 us -> 1.21 us
  starting transfers between devices: 3.79 us -> 15.9 us
  blocking collectives: 11.7 us -> 0 us
    psum x1 -> x0, waiting for transfers between devices: 348 us -> none  [device_step(): dw_sum, dws_sum = lax.psum((dw_part, dws_part), 'dp')]
    pallas_call x0 -> x10, Pallas kernels: none -> 129 us  [the longest x2 55 us: weight_sums(): pl.pallas_call(functools.partial(dw_kernel, first), grid=(10,), in_specs=...]
    conv_general_dilated x3 -> x0, matrix products: 108 us -> none  [the longest x2 57.9 us: conv_same(): lax.conv_general_dilated(left_op, right_op, (1, 1), 'SAME', dimension_num...]
    unnamed x29 -> x26, local copies, waits for them, and re-layouts: 68.8 us -> 10.4 us
    conv_general_dilated x9 -> x0, local copies, waits for them, and re-layouts: 47.7 us -> none  [conv_same(): lax.conv_general_dilated(left_op, right_op, (1, 1), 'SAME', dimension_num...]
    ppermute x2 -> x16, waiting for transfers between devices: 69.6 us -> 96.8 us  [the longest x1 36.1 us: block(): dzm_far = lax.ppermute(dzm, 'dp', swap)]
    reduce_scatter x2 -> x0, waiting for transfers between devices: 20.8 us -> none  [device_step(): lax.psum_scatter((pre_part, short_part), 'tp', scatter_dimension=3, tiled...]
    all_to_all x2 -> x0, local copies, waits for them, and re-layouts: 16.7 us -> none  [the longest x1 15.1 us: device_step(): by_channel = lax.all_to_all(act_in[0], 'tp', 3, 0, tiled=True)]
  transfers between devices with their start and end apart: 7 -> 16, of which waited for: 7 -> 7; matrix products, arithmetic and copies ran while one was open for 12% -> 3% of each run, Pallas kernels for 0% -> 33%
where the time goes in v1:
time: 258 us; the launch traced here: 254 us
  Pallas kernels  129 us (50%)
  waiting for transfers between devices  96.8 us (38%)
  starting transfers between devices  15.9 us (6%)
  local copies, waits for them, and re-layouts  10.4 us (4%)
    pallas_call x2, Pallas kernels, weight_sums(): pl.pallas_call(functools.partial(dw_kernel, first), grid=(10,), in_specs=...  55 us
    ppermute x1, waiting for transfers between devices, block(): dzm_far = lax.ppermute(dzm, 'dp', swap)  36.1 us
    ppermute x1, waiting for transfers between devices, block(): far = lax.ppermute(img, 'dp', swap)  27.4 us
    pallas_call x2, Pallas kernels, dx_half(): pl.pallas_call(dx_kernel, grid=(HALF // TILE,), in_specs=[pl.BlockSpec((G...  26.5 us
    pallas_call x1, Pallas kernels, fwd_last(): pl.pallas_call(fwd_last_kernel, grid_spec=pltpu.PrefetchScalarGridSpec(nu...  15.5 us
    ppermute x1, waiting for transfers between devices, block(): dx_peer = lax.ppermute(dx_half(g, w_peer, s_peer), 'stage', [(1, 0)])  14.5 us
    pallas_call x1, Pallas kernels, fwd_first(): pl.pallas_call(fwd_first_kernel, grid=(CH // TILE,), in_specs=[pl.BlockSp...  12.3 us
    unnamed x26, local copies, waits for them, and re-layouts  10.4 us
  transfers between devices with their start and end apart: 16, of which 7 were waited for; matrix products, arithmetic and copies ran while one was open for 3% of the time, Pallas kernels for 33%

profile of v1, /device:TPU:2, one launch (start us, length us, event | category | flops | bytes accessed | tf_op | source)
XLA Modules:
  0.0 253.9 jit_solution(10219212069963467773)
XLA Ops:
  0.6 0.0 copy-start.5
  0.6 0.0 copy-start.6
  0.7 0.0 copy-start.7
  0.7 0.0 copy-start.3
  0.7 0.0 collective-permute-start.1
  0.7 5.3 %to_blocks.2 = (bf16[784,512]{1,0:T(8,128)(2,1)}, bf16[784,512]{1,0:T(8,128)(2,1)}, bf16[784,1024]{1,0:T(8,128)(2,1)}) custom-call(s32[1]{0:T(128)} %bitcast.t_ref, bf16[1,1,28,28,1024]{4,3,2,1,0:T(8,128)(2,1)} %img_ref.2), custom_call_target="tpu_custom_call" | custom-call | flops 411041792 | bytes 3211264 | tf_op jit(solution)/shard_map/to_blocks/pallas_call | solution.py:66
  6.0 1.3 collective-permute-start.3
  7.3 0.4 collective-permute-start.2
  7.7 0.0 copy-done.5
  7.7 0.0 copy-done.6
  7.7 0.0 copy-done.7
  7.7 0.2 collective-permute-start.4
  7.9 0.0 copy-done.3
  7.9 1.6 copy.13.img_ref
  9.5 4.9 %to_blocks.3 = (bf16[784,512]{1,0:T(8,128)(2,1)}, bf16[784,512]{1,0:T(8,128)(2,1)}) custom-call(s32[1]{0:T(128)} %bitcast.t_ref, bf16[1,2,28,28,512]{4,3,2,1,0:T(8,128)(2,1)} %copy.13.img_ref), custom_call_target="tpu_custom_call" | custom-call | flops 411041792 | bytes 3211264 | tf_op jit(solution)/shard_map/to_blocks/pallas_call | solution.py:66
  14.5 0.4 collective-permute-start.5
  14.8 2.2 collective-permute-done.4
  17.1 1.3 collective-permute-start
  18.4 0.6 maximum_select_fusion.vec_ref
  19.0 9.9 %collective-permute-done.3.x_ref.refs_0_.refs_4_ = bf16[784,512]{1,0:T(8,128)(2,1)S(1)} collective-permute-done((bf16[784,512]{1,0:T(8,128)(2,1)}, bf16[784,512]{1,0:T(8,128)(2,1)S(1)}, u32[]{:S(2)}, u32[]{:S(2)}) %collective-permute-start.3) | collective-permute-done | bytes 802848 | tf_op jit(solution)/shard_map/ppermute | solution.py:417
  28.9 0.0 copy-start.4
  28.9 0.9 copy-done.4
  29.8 12.3 %fwd_first.1 = (f32[784,1024]{1,0:T(8,128)}, f32[784,1024]{1,0:T(8,128)}) custom-call(bf16[784,512]{1,0:T(8,128)(2,1)} %copy-done.4, bf16[9,512,1024]{2,1,0:T(8,128)(2,1)} %bitcast.5, bf16[512,1024]{1,0:T(8,128)(2,1)} %bitcast.8), custom_call_target="tpu_custom_call" | custom-call | flops 8220835840 | bytes 10485760 | tf_op jit(solution)/shard_map/fwd_first/pallas_call | solution.py:225
  42.1 0.0 collective-permute-done.5.dzb_ref
  42.1 0.0 copy-start.11
  42.1 3.4 %collective-permute-done.x_ref = bf16[784,512]{1,0:T(8,128)(2,1)S(1)} collective-permute-done((bf16[784,512]{1,0:T(8,128)(2,1)}, bf16[784,512]{1,0:T(8,128)(2,1)S(1)}, u32[]{:S(2)}, u32[]{:S(2)}) %collective-permute-start) | collective-permute-done | bytes 802848 | tf_op jit(solution)/shard_map/ppermute | solution.py:418
  45.5 0.0 collective-permute-done.2.s_ref
  45.5 0.0 collective-permute-done.1.w_ref
  45.5 0.0 copy-done.11
  45.5 0.9 copy-done.10
  46.4 0.3 copy-done.9
  46.7 15.5 %fwd_last.1 = (bf16[784,1024]{1,0:T(8,128)(2,1)}, bf16[784,1024]{1,0:T(8,128)(2,1)}, bf16[130,16,1024]{2,1,0:T(8,128)(2,1)}) custom-call(s32[1]{0:T(128)} %bitcast.t_ref, bf16[784,512]{1,0:T(8,128)(2,1)} %copy-done.10, bf16[9,512,1024]{2,1,0:T(8,128)(2,1)} %collective-permute-done.1.w_ref, bf16[512,1024]{1,0:T(8,128)(2,1)} %copy-done.9, ...), custom_call_target="tpu_custom_call" | custom-call | flops 8220835840 | bytes 10485760 | tf_op jit(solution)/shard_map/fwd_last/pallas_call | solution.py:244
  62.2 1.5 collective-permute-start.12
  63.8 0.0 collective-permute-start.15
  63.8 0.0 copy-done.8
  63.8 0.5 collective-permute-start.9
  64.3 36.1 %collective-permute-done.12.dzm_ref = bf16[784,1024]{1,0:T(8,128)(2,1)S(1)} collective-permute-done((bf16[784,1024]{1,0:T(8,128)(2,1)}, bf16[784,1024]{1,0:T(8,128)(2,1)S(1)}, u32[]{:S(2)}, u32[]{:S(2)}) %collective-permute-start.12) | collective-permute-done | bytes 1605664 | tf_op jit(solution)/shard_map/ppermute | solution.py:433
  100.4 1.2 copy-done.2
  101.6 4.4 %grads.1.refs_2_ = bf16[130,16,1024]{2,1,0:T(8,128)(2,1)} custom-call(bf16[784,1024]{1,0:T(8,128)(2,1)} %copy-done.2, f32[3,1024]{1,0:T(4,128)} %maximum_select_fusion.vec_ref), custom_call_target="tpu_custom_call" | custom-call | flops 6422528 | bytes 6422528 | tf_op jit(solution)/shard_map/grads/pallas_call | solution.py:282
  106.0 0.0 collective-permute-start.13
  106.0 27.4 %collective-permute-done.9 = bf16[784,1024]{1,0:T(8,128)(2,1)} collective-permute-done((bf16[784,1024]{1,0:T(8,128)(2,1)S(1)}, bf16[784,1024]{1,0:T(8,128)(2,1)}, u32[]{:S(2)}, u32[]{:S(2)}) %collective-permute-start.9) | collective-permute-done | bytes 1605664 | tf_op jit(solution)/shard_map/ppermute | solution.py:427
  133.4 1.3 collective-permute-start.10
  134.7 13.3 %dx_half.2 = bf16[784,512]{1,0:T(8,128)(2,1)} custom-call(bf16[130,16,1024]{2,1,0:T(8,128)(2,1)} %get-tuple-element.27.gh_ref.refs_2_.refs_6_.refs_7_.refs_8_.refs_9_, bf16[9,512,1024]{2,1,0:T(8,128)(2,1)} %bitcast.6, bf16[512,1024]{1,0:T(8,128)(2,1)} %bitcast.9), custom_call_target="tpu_custom_call" | custom-call | flops 8220835840 | bytes 10485760 | tf_op jit(solution)/shard_map/dx_half/pallas_call | solution.py:307
  147.9 6.7 %collective-permute-start.7 = (bf16[784,512]{1,0:T(8,128)(2,1)}, bf16[784,512]{1,0:T(8,128)(2,1)}, u32[]{:S(2)}, u32[]{:S(2)}) collective-permute-start(bf16[784,512]{1,0:T(8,128)(2,1)} %dx_half.2), channel_id=1, source_target_pairs={{2,0},{3,1},{6,4},{7,5}} | collective-permute-start | bytes 2408456 | tf_op jit(solution)/shard_map/ppermute | solution.py:436
  154.6 0.0 copy-done
  154.6 0.0 collective-permute-start.6
  154.6 13.3 %dx_half.3 = bf16[784,512]{1,0:T(8,128)(2,1)} custom-call(bf16[130,16,1024]{2,1,0:T(8,128)(2,1)} %get-tuple-element.27.gh_ref.refs_2_.refs_6_.refs_7_.refs_8_.refs_9_, bf16[9,512,1024]{2,1,0:T(8,128)(2,1)} %collective-permute-done.1.w_ref, bf16[512,1024]{1,0:T(8,128)(2,1)} %copy-done.9), custom_call_target="tpu_custom_call" | custom-call | flops 8220835840 | bytes 10485760 | tf_op jit(solution)/shard_map/dx_half/pallas_call | solution.py:307
  167.9 3.2 %collective-permute-done.10.refs_0_ = bf16[784,1024]{1,0:T(8,128)(2,1)} collective-permute-done((bf16[784,1024]{1,0:T(8,128)(2,1)}, bf16[784,1024]{1,0:T(8,128)(2,1)}, u32[]{:S(2)}, u32[]{:S(2)}) %collective-permute-start.10) | collective-permute-done | bytes 1605664 | tf_op jit(solution)/shard_map/ppermute | solution.py:428
  171.1 2.4 collective-permute-start.8
  173.5 0.0 collective-permute-done.7.dx_own_ref
  173.5 0.0 collective-permute-start.14
  173.5 14.5 %collective-permute-done.8.dx_peer_ref = bf16[784,512]{1,0:T(8,128)(2,1)} collective-permute-done((bf16[784,512]{1,0:T(8,128)(2,1)}, bf16[784,512]{1,0:T(8,128)(2,1)}, u32[]{:S(2)}, u32[]{:S(2)}) %collective-permute-start.8) | collective-permute-done | bytes 802848 | tf_op jit(solution)/shard_map/ppermute | solution.py:437
  188.0 0.0 collective-permute-start.11
  188.0 0.6 pad_add_fusion.idx_ref
  188.6 0.0 collective-permute-done.6.z_near_ref
  188.6 1.2 copy-done.1
  189.8 4.8 %from_blocks.1 = (bf16[1,2,28,28,512]{4,3,2,1,0:T(8,128)(2,1)}, bf16[1,1,28,28,1024]{4,3,2,1,0:T(8,128)(2,1)}) custom-call(s32[2]{0:T(128)} %pad_add_fusion.idx_ref, bf16[784,1024]{1,0:T(8,128)(2,1)} %get-tuple-element.26.z_ref, bf16[784,1024]{1,0:T(8,128)(2,1)} %copy-done.1, bf16[784,512]{1,0:T(8,128)(2,1)} %collective-permute-done.7.dx_own_ref, ...), custom_call_target="tpu_custom_call" | custom-call | flops 411041792 | bytes 6422528 | tf_op jit(solution)/shard_map/from_blocks/pallas_call | solution.py:120
  194.6 4.3 %copy.14 = bf16[1,2,28,28,512]{4,1,3,2,0:T(2,128)(2,1)} copy(bf16[1,2,28,28,512]{4,3,2,1,0:T(8,128)(2,1)} %get-tuple-element.36) | data formatting | bytes 3211264
  198.9 0.0 collective-permute-done.14.refs_1_.refs_5_
  198.9 0.0 collective-permute-done.15.refs_3_.refs_10_.refs_11_.refs_12_.refs_13_
  198.9 25.0 %weight_sums.2 = (f32[1,3,3,512,1024]{4,3,2,1,0:T(8,128)}, f32[1,512,1024]{2,1,0:T(8,128)}) custom-call(bf16[784,512]{1,0:T(8,128)(2,1)} %copy-done.4, bf16[784,512]{1,0:T(8,128)(2,1)} %collective-permute-done.14.refs_1_.refs_5_, bf16[130,16,1024]{2,1,0:T(8,128)(2,1)} %get-tuple-element.27.gh_ref.refs_2_.refs_6_.refs_7_.refs_8_.refs_9_, ...), custom_call_target="tpu_custom_call" | custom-call | flops 16441671680 | bytes 20971520 | tf_op jit(solution)/shard_map/weight_sums/pallas_call | solution.py:387
  223.9 0.0 collective-permute-done.11.refs_1_
  223.9 0.0 collective-permute-done.13.refs_3_
  223.9 30.0 %weight_sums.3 = (f32[1,3,3,512,1024]{4,3,2,1,0:T(8,128)}, f32[1,512,1024]{2,1,0:T(8,128)}) custom-call(bf16[784,1024]{1,0:T(8,128)(2,1)} %collective-permute-done.10.refs_0_, bf16[784,1024]{1,0:T(8,128)(2,1)} %collective-permute-done.11.refs_1_, bf16[130,16,1024]{2,1,0:T(8,128)(2,1)} %grads.1.refs_2_, ...), custom_call_target="tpu_custom_call", output_to_operand_aliasing={{0}: (14, {}), {1}: (15, {})} | custom-call | flops 16441671680 | bytes 20971520 | tf_op jit(solution)/shard_map/weight_sums/pallas_call | solution.py:387
  (7 shorter events, 0.0 us)
Async XLA Ops:
  0.6 7.1 %copy-start.5 = (f32[1,512]{1,0:T(1,128)S(1)}, f32[1,512]{1,0:T(1,128)}, u32[]{:S(2)}) copy-start(f32[1,512]{1,0:T(1,128)} %param.12) | copy-start | bytes 6148
  0.6 7.1 %copy-start.6 = (f32[1,512]{1,0:T(1,128)S(1)}, f32[1,512]{1,0:T(1,128)}, u32[]{:S(2)}) copy-start(f32[1,512]{1,0:T(1,128)} %param.11) | copy-start | bytes 6148
  0.7 7.1 %copy-start.7 = (f32[1,512]{1,0:T(1,128)S(1)}, f32[1,512]{1,0:T(1,128)}, u32[]{:S(2)}) copy-start(f32[1,512]{1,0:T(1,128)} %param.10) | copy-start | bytes 6148
  0.7 7.2 %copy-start.3 = (bf16[1,2,28,28,512]{4,1,3,2,0:T(2,128)(2,1)S(1)}, bf16[1,2,28,28,512]{4,1,3,2,0:T(2,128)(2,1)}, u32[]{:S(2)}) copy-start(bf16[1,2,28,28,512]{4,1,3,2,0:T(2,128)(2,1)} %param.13) | copy-start | bytes 4816900
  0.7 44.8 %collective-permute-start.1 = (bf16[9,512,1024]{2,1,0:T(8,128)(2,1)}, bf16[9,512,1024]{2,1,0:T(8,128)(2,1)}, u32[]{:S(2)}, u32[]{:S(2)}) collective-permute-start(bf16[9,512,1024]{2,1,0:T(8,128)(2,1)} %bitcast.4), channel_id=1, source_target_pairs={{0,1},{1,0},{2,3},{3,2},{4,5},{5,4},{6,7},{7,6}} | collective-permute-start | bytes 28311560 | tf_op jit(solution)/shard_map/ppermute | solution.py:419
  6.0 22.9 %collective-permute-start.3 = (bf16[784,512]{1,0:T(8,128)(2,1)}, bf16[784,512]{1,0:T(8,128)(2,1)S(1)}, u32[]{:S(2)}, u32[]{:S(2)}) collective-permute-start(bf16[784,512]{1,0:T(8,128)(2,1)} %get-tuple-element.21), channel_id=1, source_target_pairs={{0,2},{1,3},{4,6},{5,7}} | collective-permute-start | bytes 2408456 | tf_op jit(solution)/shard_map/ppermute | solution.py:417
  7.3 38.2 %collective-permute-start.2 = (bf16[512,1024]{1,0:T(8,128)(2,1)}, bf16[512,1024]{1,0:T(8,128)(2,1)S(1)}, u32[]{:S(2)}, u32[]{:S(2)}) collective-permute-start(bf16[512,1024]{1,0:T(8,128)(2,1)} %bitcast.7), channel_id=1, source_target_pairs={{0,1},{1,0},{2,3},{3,2},{4,5},{5,4},{6,7},{7,6}} | collective-permute-start | bytes 3145736 | tf_op jit(solution)/shard_map/ppermute | solution.py:420
  7.7 9.3 %collective-permute-start.4 = (f32[3,512]{1,0:T(4,128)S(1)}, f32[3,512]{1,0:T(4,128)S(1)}, u32[]{:S(2)}, u32[]{:S(2)}) collective-permute-start(f32[3,512]{1,0:T(4,128)S(1)} %pad_maximum_fusion), channel_id=1, source_target_pairs={{0,1},{1,0},{2,3},{3,2},{4,5},{5,4},{6,7},{7,6}} | collective-permute-start | bytes 18440 | tf_op jit(solution)/shard_map/ppermute | solution.py:422
  14.5 27.6 %collective-permute-start.5 = (bf16[784,512]{1,0:T(8,128)(2,1)}, bf16[784,512]{1,0:T(8,128)(2,1)S(1)}, u32[]{:S(2)}, u32[]{:S(2)}) collective-permute-start(bf16[784,512]{1,0:T(8,128)(2,1)} %get-tuple-element.25), channel_id=1, source_target_pairs={{0,1},{1,0},{2,3},{3,2},{4,5},{5,4},{6,7},{7,6}} | collective-permute-start | bytes 2408456 | tf_op jit(solution)/shard_map/ppermute | solution.py:425
  17.1 28.4 %collective-permute-start = (bf16[784,512]{1,0:T(8,128)(2,1)}, bf16[784,512]{1,0:T(8,128)(2,1)S(1)}, u32[]{:S(2)}, u32[]{:S(2)}) collective-permute-start(bf16[784,512]{1,0:T(8,128)(2,1)} %get-tuple-element.20), channel_id=1, source_target_pairs={{0,2},{1,3},{4,6},{5,7}} | collective-permute-start | bytes 2408456 | tf_op jit(solution)/shard_map/ppermute | solution.py:418
  28.9 0.9 copy-start.4
  42.1 3.4 %copy-start.11 = (bf16[784,512]{1,0:T(8,128)(2,1)}, bf16[784,512]{1,0:T(8,128)(2,1)S(1)}, u32[]{:S(2)}) copy-start(bf16[784,512]{1,0:T(8,128)(2,1)S(1)} %collective-permute-done.5.dzb_ref) | copy-start | bytes 2408452
  45.5 0.9 copy-start.10
  45.5 1.2 copy-start.9
  46.7 17.0 %copy-start.8 = (bf16[784,1024]{1,0:T(8,128)(2,1)S(1)}, bf16[784,1024]{1,0:T(8,128)(2,1)}, u32[]{:S(2)}) copy-start(bf16[784,1024]{1,0:T(8,128)(2,1)} %get-tuple-element.30) | copy-start | bytes 4816900
  62.2 38.2 %collective-permute-start.12 = (bf16[784,1024]{1,0:T(8,128)(2,1)}, bf16[784,1024]{1,0:T(8,128)(2,1)S(1)}, u32[]{:S(2)}, u32[]{:S(2)}) collective-permute-start(bf16[784,1024]{1,0:T(8,128)(2,1)} %get-tuple-element.31), channel_id=1, source_target_pairs={{0,4},{4,0},{1,5},{5,1},{2,6},{6,2},{3,7},{7,3}} | collective-permute-start | bytes 4816904 | tf_op jit(solution)/shard_map/ppermute | solution.py:433
  63.8 135.2 %collective-permute-start.15 = (bf16[130,16,1024]{2,1,0:T(8,128)(2,1)}, bf16[130,16,1024]{2,1,0:T(8,128)(2,1)}, u32[]{:S(2)}, u32[]{:S(2)}) collective-permute-start(bf16[130,16,1024]{2,1,0:T(8,128)(2,1)} %get-tuple-element.27.gh_ref.refs_2_.refs_6_.refs_7_.refs_8_.refs_9_), channel_id=1, source_target_pairs={{0,1},{1,0},{2,3},{3,2},{4,5},{5,4},{6,7},{7,6}} | collective-permute-start | bytes 12779528 | tf_op jit(solution)/shard_map/ppermute | solution.py:434
  63.8 69.6 %collective-permute-start.9 = (bf16[784,1024]{1,0:T(8,128)(2,1)S(1)}, bf16[784,1024]{1,0:T(8,128)(2,1)}, u32[]{:S(2)}, u32[]{:S(2)}) collective-permute-start(bf16[784,1024]{1,0:T(8,128)(2,1)S(1)} %copy-done.8), channel_id=1, source_target_pairs={{0,4},{4,0},{1,5},{5,1},{2,6},{6,2},{3,7},{7,3}} | collective-permute-start | bytes 4816904 | tf_op jit(solution)/shard_map/ppermute | solution.py:427
  100.4 1.2 copy-start.2
  106.0 48.6 %copy-start = (bf16[784,1024]{1,0:T(8,128)(2,1)S(1)}, bf16[784,1024]{1,0:T(8,128)(2,1)}, u32[]{:S(2)}) copy-start(bf16[784,1024]{1,0:T(8,128)(2,1)} %get-tuple-element.26.z_ref) | copy-start | bytes 4816900
  106.0 117.9 %collective-permute-start.13 = (bf16[130,16,1024]{2,1,0:T(8,128)(2,1)}, bf16[130,16,1024]{2,1,0:T(8,128)(2,1)}, u32[]{:S(2)}, u32[]{:S(2)}) collective-permute-start(bf16[130,16,1024]{2,1,0:T(8,128)(2,1)} %grads.1.refs_2_), channel_id=1, source_target_pairs={{0,1},{1,0},{2,3},{3,2},{4,5},{5,4},{6,7},{7,6}} | collective-permute-start | bytes 12779528 | tf_op jit(solution)/shard_map/ppermute | solution.py:440
  133.4 37.8 %collective-permute-start.10 = (bf16[784,1024]{1,0:T(8,128)(2,1)}, bf16[784,1024]{1,0:T(8,128)(2,1)}, u32[]{:S(2)}, u32[]{:S(2)}) collective-permute-start(bf16[784,1024]{1,0:T(8,128)(2,1)} %collective-permute-done.9), channel_id=1, source_target_pairs={{0,2},{1,3},{4,6},{5,7}} | collective-permute-start | bytes 4816904 | tf_op jit(solution)/shard_map/ppermute | solution.py:428
  147.9 25.6 %collective-permute-start.7 = (bf16[784,512]{1,0:T(8,128)(2,1)}, bf16[784,512]{1,0:T(8,128)(2,1)}, u32[]{:S(2)}, u32[]{:S(2)}) collective-permute-start(bf16[784,512]{1,0:T(8,128)(2,1)} %dx_half.2), channel_id=1, source_target_pairs={{2,0},{3,1},{6,4},{7,5}} | collective-permute-start | bytes 2408456 | tf_op jit(solution)/shard_map/ppermute | solution.py:436
  154.6 34.0 %collective-permute-start.6 = (bf16[784,1024]{1,0:T(8,128)(2,1)S(1)}, bf16[784,1024]{1,0:T(8,128)(2,1)S(1)}, u32[]{:S(2)}, u32[]{:S(2)}) collective-permute-start(bf16[784,1024]{1,0:T(8,128)(2,1)S(1)} %copy-done), channel_id=1, source_target_pairs={{0,1},{1,0},{2,3},{3,2},{4,5},{5,4},{6,7},{7,6}} | collective-permute-start | bytes 4816904 | tf_op jit(solution)/shard_map/ppermute | solution.py:435
  171.1 16.9 %collective-permute-start.8 = (bf16[784,512]{1,0:T(8,128)(2,1)}, bf16[784,512]{1,0:T(8,128)(2,1)}, u32[]{:S(2)}, u32[]{:S(2)}) collective-permute-start(bf16[784,512]{1,0:T(8,128)(2,1)} %dx_half.3), channel_id=1, source_target_pairs={{2,0},{3,1},{6,4},{7,5}} | collective-permute-start | bytes 2408456 | tf_op jit(solution)/shard_map/ppermute | solution.py:437
  173.5 25.4 %collective-permute-start.14 = (bf16[784,512]{1,0:T(8,128)(2,1)}, bf16[784,512]{1,0:T(8,128)(2,1)}, u32[]{:S(2)}, u32[]{:S(2)}) collective-permute-start(bf16[784,512]{1,0:T(8,128)(2,1)} %copy-done.10), channel_id=1, source_target_pairs={{0,1},{1,0},{2,3},{3,2},{4,5},{5,4},{6,7},{7,6}} | collective-permute-start | bytes 2408456 | tf_op jit(solution)/shard_map/ppermute | solution.py:431
  188.0 35.9 %collective-permute-start.11 = (bf16[784,1024]{1,0:T(8,128)(2,1)}, bf16[784,1024]{1,0:T(8,128)(2,1)}, u32[]{:S(2)}, u32[]{:S(2)}) collective-permute-start(bf16[784,1024]{1,0:T(8,128)(2,1)} %collective-permute-done.10.refs_0_), channel_id=1, source_target_pairs={{0,1},{1,0},{2,3},{3,2},{4,5},{5,4},{6,7},{7,6}} | collective-permute-start | bytes 4816904 | tf_op jit(solution)/shard_map/ppermute | solution.py:438
  188.6 1.2 copy-start.1

commit v2 on v1

v2 whole, which is shorter than its diff:
```python
import functools

import jax
import jax.numpy as jnp
from jax import lax
from jax.experimental import pallas as pl
from jax.experimental.pallas import tpu as pltpu
from jax.sharding import PartitionSpec as P


SIDE = 28
LO = 7
GRP = 16
HAL = LO + 2
GROUPS = HAL * HAL + LO * LO
PIX = SIDE * SIDE
HALF = 512
CH = 1024
TILE = 256
F32 = jnp.float32
BF16 = jnp.bfloat16
VMEM_LIMIT = 60 * 1024 * 1024


def params(n_axes):
    return pltpu.CompilerParams(dimension_semantics=("arbitrary",) * n_axes, vmem_limit_bytes=VMEM_LIMIT)


def cost(flops, bytes_accessed):
    return pl.CostEstimate(flops=int(flops), bytes_accessed=int(bytes_accessed), transcendentals=0)


def order_matrix(transposed):
    shape = (128, 112) if transposed else (112, 128)
    row = lax.broadcasted_iota(jnp.int32, shape, 1 if transposed else 0)
    col = lax.broadcasted_iota(jnp.int32, shape, 0 if transposed else 1)
    w_lo, h_hi, w_hi = row // 16, (row // 4) % 4, row % 4
    return (col == h_hi * 32 + w_hi * 7 + w_lo).astype(F32).astype(BF16)


def from_blocks_kernel(idx_ref, z_ref, z_near_ref, dx_own_ref, dx_peer_ref, z_out, dx_out):
    select = order_matrix(True)
    step = pl.program_id(0)
    stage = idx_ref[1]

    def emit(ref, out_ref):
        for lo in range(LO):
            rows = jnp.dot(select, ref[lo * 112:(lo + 1) * 112, :], preferred_element_type=F32).astype(BF16)
            for hi in range(4):
                out_ref[hi * LO + lo] = rows[hi * 32:hi * 32 + SIDE, :]

    @pl.when(stage == 0)
    def _():
        z_out[...] = jnp.zeros_like(z_out)

        @pl.when(step == 0)
        def _():
            emit(dx_own_ref, dx_out)

        @pl.when(step == 1)
        def _():
            emit(dx_peer_ref, dx_out)

    @pl.when(stage == 1)
    def _():
        dx_out[...] = jnp.zeros_like(dx_out)

        @pl.when(step == 0)
        def _():
            emit(z_ref, z_out)

        @pl.when(step == 1)
        def _():
            emit(z_near_ref, z_out)


def from_blocks(idx, z, z_near, dx_own, dx_peer):
    return pl.pallas_call(
        from_blocks_kernel,
        grid_spec=pltpu.PrefetchScalarGridSpec(
            num_scalar_prefetch=1,
            grid=(2,),
            in_specs=[
                pl.BlockSpec((PIX, HALF), lambda k, m: (0, 0)),
                pl.BlockSpec((PIX, HALF), lambda k, m: (0, 1)),
                pl.BlockSpec((PIX, HALF), lambda k, m: (0, 0)),
                pl.BlockSpec((PIX, HALF), lambda k, m: (0, 0)),
            ],
            out_specs=[
                pl.BlockSpec((None, None, SIDE, SIDE, HALF), lambda k, m: (0, (m[0] + k) % 2, 0, 0, 0)),
                pl.BlockSpec((None, None, SIDE, SIDE, HALF), lambda k, m: (0, 0, 0, 0, (m[0] + k) % 2)),
            ],
        ),
        out_shape=[
            jax.ShapeDtypeStruct((1, 2, SIDE, SIDE, HALF), BF16),
            jax.ShapeDtypeStruct((1, 1, SIDE, SIDE, CH), BF16),
        ],
        compiler_params=params(1),
        cost_estimate=cost(2 * 2 * 7 * 112 * 128 * HALF * 2, 4 * 2 * PIX * HALF * 2),
        name="from_blocks",
    )(idx, z, z_near, dx_own, dx_peer)


def moved(tile, step_h, step_w):
    wide = tile.astype(F32)
    n = wide.shape[1]
    if step_h < 0:
        wide = jnp.concatenate([jnp.zeros((4, n), F32), wide[:12]], axis=0)
    if step_h > 0:
        wide = jnp.concatenate([wide[4:], jnp.zeros((4, n), F32)], axis=0)
    if step_w:
        w_hi = lax.broadcasted_iota(jnp.int32, (GRP, n), 0) % 4
        if step_w < 0:
            wide = jnp.concatenate([wide[15:], wide[:15]], axis=0)
            wide = jnp.where(w_hi == 0, 0.0, wide)
        else:
            wide = jnp.concatenate([wide[1:], wide[:1]], axis=0)
            wide = jnp.where(w_hi == 3, 0.0, wide)
    return wide.astype(BF16)


def fill_halo(dst_ref, value):
    n = value.shape[1]
    groups = value.reshape(LO, LO, GRP, n)
    for a in range(HAL):
        step_h = -1 if a == 0 else (1 if a == HAL - 1 else 0)
        if not step_h:
            dst_ref[a * HAL + 1:a * HAL + 1 + LO] = groups[a - 1]
        for b in range(HAL):
            step_w = -1 if b == 0 else (1 if b == HAL - 1 else 0)
            if step_h or step_w:
                dst_ref[a * HAL + b] = moved(groups[(a - 1) % LO, (b - 1) % LO], step_h, step_w)


def window(ref, i, j):
    parts = [ref[pl.ds((i + a) * HAL + j, LO)] for a in range(LO)]
    whole = jnp.concatenate(parts, axis=0)
    return whole.reshape(PIX, whole.shape[-1])


def both_grads(dz, vec_ref, g_ref):
    g_ref[HAL * HAL:] = (dz * vec_ref[2:3, :]).astype(BF16).reshape(LO * LO, GRP, -1)
    fill_halo(g_ref, (dz * vec_ref[0:1, :]).astype(BF16))


FWD_FLOPS = 2 * PIX * HALF * CH * 10
W_BYTES = 10 * HALF * CH * 2


def grads_kernel(dzm_ref, vec_ref, g_ref):
    both_grads(dzm_ref[...].astype(F32), vec_ref, g_ref)


def grads(dzm, vec):
    return pl.pallas_call(
        grads_kernel,
        grid=(CH // TILE,),
        in_specs=[pl.BlockSpec((PIX, TILE), lambda j: (0, j)), pl.BlockSpec((3, TILE), lambda j: (0, j))],
        out_specs=pl.BlockSpec((GROUPS, GRP, TILE), lambda j: (0, 0, j)),
        out_shape=jax.ShapeDtypeStruct((GROUPS, GRP, CH), BF16),
        compiler_params=params(1),
        cost_estimate=cost(8 * PIX * CH, 8 * PIX * CH),
        name="grads",
    )(dzm, vec)


CHUNK = 256
N_CHUNKS = CH // CHUNK
MESH = pl.DeviceIdType.MESH


def arrange(src, pad_ref, select, dst):
    pad_ref[:, :SIDE, :] = src
    for lo in range(LO):
        rows = jnp.concatenate([pad_ref[hi * LO + lo] for hi in range(4)], axis=0)
        dst[lo * 112:(lo + 1) * 112, :] = jnp.dot(select, rows, preferred_element_type=F32).astype(BF16)


def front_kernel(
    act, grad, gam, bet, gms, w_own, s_own,
    x_own, x_near, img_far, w_peer, s_peer, vec_out, z_out, dzm_out, g_out,
    pad_c, pad_h, xs, xr, xh, im, w_buf, s_buf, pre, short, dz_own, dz_send, dz_peer, vec_peer, z_st, dzm_st, g_st,
    x_send, x_recv, far_send, far_recv, near_send, near_recv, w_send, w_recv, vec_send, vec_recv, dz_sem, dz_rsem, w_local, x_local, out_sem, vec_sem,
):
    t = lax.axis_index("tp")
    stage = lax.axis_index("stage")
    dp = lax.axis_index("dp")

    barrier = pltpu.get_barrier_semaphore()
    for target in ({"tp": 1 - t}, {"stage": 1 - stage}, {"dp": 1 - dp}):
        pl.semaphore_signal(barrier, inc=1, device_id=target, device_id_type=MESH)
    pl.semaphore_wait(barrier, 3)

    def remote(src, dst, send, recv, target):
        return pltpu.make_async_remote_copy(src_ref=src, dst_ref=dst, send_sem=send, recv_sem=recv, device_id=target, device_id_type=MESH)

    peer = {"tp": 1 - t}

    def x_copy(q):
        return remote(xs.at[q], xr.at[q], x_send.at[q], x_recv.at[q], {"stage": 1 - stage})

    def far_copy(q):
        return remote(xs.at[q], img_far.at[q], far_send.at[q], far_recv.at[q], {"dp": 1 - dp})

    def near_copy(q):
        return remote(xr.at[q], x_near.at[q - 2], near_send.at[q - 2], near_recv.at[q - 2], peer)

    def keep_copy(q):
        return pltpu.make_async_copy(xr.at[q], x_own.at[q], x_local.at[q])

    @pl.when(stage == 0)
    def _():
        pad_c[...] = jnp.zeros_like(pad_c)
        select = order_matrix(False)
        for q in range(N_CHUNKS):
            col = pl.multiple_of(lax.rem(t * HALF + q * CHUNK, CH), CHUNK)
            arrange(act[0, 0, :, :, pl.ds(col, CHUNK)], pad_c, select, xs.at[q])
            x_copy(q).start()
            far_copy(q).start()
        for q in range(N_CHUNKS):
            x_copy(q).wait_send()
            far_copy(q).wait_send()
            far_copy(q).wait_recv()

    @pl.when(stage == 1)
    def _():
        w_copy = remote(w_own, w_peer, w_send.at[0], w_recv.at[0], peer)
        s_copy = remote(s_own, s_peer, w_send.at[1], w_recv.at[1], peer)
        vec_copies = [remote(ref, vec_peer.at[k], vec_send.at[k], vec_recv.at[k], peer) for k, ref in enumerate((gam, bet, gms))]
        w_copy.start()
        s_copy.start()
        for copy in vec_copies:
            copy.start()

        def w_fetch(src_w, src_s, block, q):
            rows = pl.ds(block * CHUNK, CHUNK)
            return (
                pltpu.make_async_copy(src_w.at[:, rows], w_buf.at[q], w_local.at[q, 0]),
                pltpu.make_async_copy(src_s.at[rows], s_buf.at[q], w_local.at[q, 1]),
            )

        for q in range(2):
            for copy in w_fetch(w_own, s_own, q, q):
                copy.start()

        pad_h[...] = jnp.zeros_like(pad_h)
        select = order_matrix(False)
        arrange(grad[0, 1 - t], pad_h, select, dz_send)
        dz_copy = remote(dz_send, dz_peer, dz_sem, dz_rsem, peer)
        dz_copy.start()
        arrange(grad[0, t], pad_h, select, dz_own)

        def chunk(q, carry):
            x_copy(q).wait_recv()

            @pl.when(q < 2)
            def _():
                keep_copy(q).start()

            @pl.when(q >= 2)
            def _():
                near_copy(q).start()

            fill_halo(xh, xr[q])
            for i in range(3):
                for j in range(3):
                    k = i * 3 + j
                    im[:, k * CHUNK:(k + 1) * CHUNK] = window(xh, i, j)

            @pl.when(q == 1)
            def _():
                w_copy.wait_recv()
                s_copy.wait_recv()
                for k in range(2):
                    for copy in w_fetch(w_peer, s_peer, k, k + 2):
                        copy.start()

            for copy in w_fetch(w_own, s_own, 0, q):
                copy.wait()
            for n in range(2):
                cols = slice(n * HALF, (n + 1) * HALF)
                main = jnp.dot(im[...], w_buf[q, :, :, cols].reshape(9 * CHUNK, HALF), preferred_element_type=F32)
                side = jnp.dot(xr[q], s_buf[q, :, cols], preferred_element_type=F32)

                @pl.when(q == 0)
                def _():
                    pre[:, cols] = main
                    short[:, cols] = side

                @pl.when(q > 0)
                def _():
                    pre[:, cols] += main
                    short[:, cols] += side

            return carry

        lax.fori_loop(0, N_CHUNKS, chunk, 0)

        for copy in vec_copies:
            copy.wait_recv()
        dz_copy.wait_recv()
        outs = []
        for n in range(CH // TILE):
            half, part = n // 2, slice((n % 2) * TILE, (n % 2 + 1) * TILE)
            cols = slice(n * TILE, (n + 1) * TILE)
            mine = t == half
            gamma, beta, gamma_s = (jnp.where(mine, ref[:, part], vec_peer[k, :, part]) for k, ref in enumerate((gam, bet, gms)))
            for k, row in enumerate((gamma, beta, gamma_s)):
                vec_out[k:k + 1, cols] = row
            u = pre[:, cols] * gamma + beta + short[:, cols] * gamma_s
            z_st[:, cols] = jnp.maximum(u, 0.0).astype(BF16)
            dz = jnp.where(mine, dz_own[:, part].astype(F32), dz_peer[:, part].astype(F32))
            dz = jnp.where(u > 0.0, dz, 0.0)
            dzm_st[:, cols] = dz.astype(BF16)
            g_st[HAL * HAL:, :, cols] = (dz * gamma_s).astype(BF16).reshape(LO * LO, GRP, TILE)
            fill_halo(g_st.at[:, :, cols], (dz * gamma).astype(BF16))
            to = pl.multiple_of(lax.rem(n * TILE + t * HALF, CH), TILE)
            outs.append(pltpu.make_async_copy(z_st.at[:, cols], z_out.at[:, pl.ds(to, TILE)], out_sem.at[n, 0]))
            outs.append(pltpu.make_async_copy(dzm_st.at[:, cols], dzm_out.at[:, cols], out_sem.at[n, 1]))
            outs.append(pltpu.make_async_copy(g_st.at[:, :, cols], g_out.at[:, :, cols], out_sem.at[n, 2]))
            for copy in outs[-3:]:
                copy.start()

        for copy in outs:
            copy.wait()
        for q in range(2):
            keep_copy(q).wait()
            near_copy(q + 2).wait_send()
            near_copy(q + 2).wait_recv()
        for copy in [w_copy, s_copy, dz_copy] + vec_copies:
            copy.wait_send()


def front(act_in, grad_z, gamma, beta, gamma_s, w_own, s_own):
    vmem = pl.BlockSpec(memory_space=pltpu.VMEM)
    anywhere = pl.BlockSpec(memory_space=pl.ANY)
    dma = pltpu.SemaphoreType.DMA
    chunks = (N_CHUNKS, PIX, CHUNK)
    return pl.pallas_call(
        front_kernel,
        in_specs=[vmem] * 5 + [anywhere] * 2,
        out_specs=[anywhere] * 5 + [vmem] + [anywhere] * 3,
        out_shape=[
            jax.ShapeDtypeStruct((2, PIX, CHUNK), BF16),
            jax.ShapeDtypeStruct((2, PIX, CHUNK), BF16),
            jax.ShapeDtypeStruct(chunks, BF16),
            jax.ShapeDtypeStruct((9, HALF, CH), BF16),
            jax.ShapeDtypeStruct((HALF, CH), BF16),
            jax.ShapeDtypeStruct((3, CH), F32),
            jax.ShapeDtypeStruct((PIX, CH), BF16),
            jax.ShapeDtypeStruct((PIX, CH), BF16),
            jax.ShapeDtypeStruct((GROUPS, GRP, CH), BF16),
        ],
        scratch_shapes=[
            pltpu.VMEM((SIDE, 32, CHUNK), BF16),
            pltpu.VMEM((SIDE, 32, HALF), BF16),
            pltpu.VMEM(chunks, BF16),
            pltpu.VMEM(chunks, BF16),
            pltpu.VMEM((HAL * HAL, GRP, CHUNK), BF16),
            pltpu.VMEM((PIX, 9 * CHUNK), BF16),
            pltpu.VMEM((N_CHUNKS, 9, CHUNK, CH), BF16),
            pltpu.VMEM((N_CHUNKS, CHUNK, CH), BF16),
            pltpu.VMEM((PIX, CH), F32),
            pltpu.VMEM((PIX, CH), F32),
            pltpu.VMEM((PIX, HALF), BF16),
            pltpu.VMEM((PIX, HALF), BF16),
            pltpu.VMEM((PIX, HALF), BF16),
            pltpu.VMEM((3, 1, HALF), F32),
            pltpu.VMEM((PIX, CH), BF16),
            pltpu.VMEM((PIX, CH), BF16),
            pltpu.VMEM((GROUPS, GRP, CH), BF16),
            dma((4,)), dma((4,)), dma((4,)), dma((4,)), dma((2,)), dma((2,)), dma((2,)), dma((2,)), dma((3,)), dma((3,)),
            dma, dma, dma((4, 2)), dma((2,)), dma((4, 3)), dma((1,)),
        ],
        compiler_params=pltpu.CompilerParams(collective_id=0, has_side_effects=True, vmem_limit_bytes=66 * 1000 * 1000),
        cost_estimate=cost(2 * FWD_FLOPS, 2 * W_BYTES),
        name="front",
    )(act_in, grad_z, gamma, beta, gamma_s, w_own, s_own)


def dot_nt(a, b):
    return lax.dot_general(a, b, (((1,), (1,)), ((), ())), preferred_element_type=F32)


def dx_kernel(gh_ref, w_ref, s_ref, dx_ref):
    total = dot_nt(gh_ref[HAL * HAL:].reshape(PIX, CH), s_ref[...])
    for i in range(3):
        for j in range(3):
            total = total + dot_nt(window(gh_ref, 2 - i, 2 - j), w_ref[i * 3 + j])
    dx_ref[...] = total.astype(BF16)


def dx_half(g, w, s):
    return pl.pallas_call(
        dx_kernel,
        grid=(HALF // TILE,),
        in_specs=[
            pl.BlockSpec((GROUPS, GRP, CH), lambda j: (0, 0, 0)),
            pl.BlockSpec((9, TILE, CH), lambda j: (0, j, 0)),
            pl.BlockSpec((TILE, CH), lambda j: (j, 0)),
        ],
        out_specs=pl.BlockSpec((PIX, TILE), lambda j: (0, j)),
        out_shape=jax.ShapeDtypeStruct((PIX, HALF), BF16),
        compiler_params=params(1),
        cost_estimate=cost(FWD_FLOPS, W_BYTES),
        name="dx_half",
    )(g, w, s)


MAIN = 768


def dw_kernel(first, idx_ref, *refs):
    if first:
        xa_ref, xb_ref, ga_ref, gb_ref, dw_ref, ds_ref, xt_ref = refs
    else:
        xa_ref, xb_ref, ga_ref, gb_ref = refs[:4]
        x_tails, g_tails = refs[4:6], (refs[6:10], refs[10:14])
        dw_in, ds_in, dw_ref, ds_ref, xt_ref = refs[14:]
    step = pl.program_id(0)

    stage = idx_ref[1]

    @pl.when((step == 0) & (stage == 1))
    def _():
        for q in range(2):
            rows = slice(q * CHUNK, (q + 1) * CHUNK)
            xt_ref[rows, :MAIN] = xa_ref[q, :MAIN, :].T
            xt_ref[rows, MAIN:2 * MAIN] = xb_ref[q, :MAIN, :].T
            if not first:
                ends = [xa_ref[q, MAIN:, :], xb_ref[q, MAIN:, :]] + [ref[q] for ref in x_tails]
                xt_ref[rows, 2 * MAIN:] = jnp.concatenate(ends, axis=0).T

    @pl.when(stage == 0)
    def _():
        dw_ref[...] = jnp.zeros_like(dw_ref)
        ds_ref[...] = jnp.zeros_like(ds_ref)

    def product(a, b, tails):
        parts = [a[:MAIN], b[:MAIN]]
        if not first:
            parts += [a[MAIN:], b[MAIN:]] + tails
        return jnp.dot(xt_ref[...], jnp.concatenate(parts, axis=0), preferred_element_type=F32)

    @pl.when((step < 9) & (stage == 1))
    def _():
        i, j = 2 - step // 3, 2 - step % 3
        tails = []
        if not first:
            for rows in g_tails:
                tail = rows[0][j]
                tail = jnp.where(i == 1, rows[1][j], tail)
                tails.append(jnp.where(i == 2, rows[2][j], tail))
        total = product(window(ga_ref, i, j), window(gb_ref, i, j), tails)
        dw_ref[...] = total if first else total + dw_in[...]

    @pl.when((step == 9) & (stage == 1))
    def _():
        tails = [] if first else [rows[3][0] for rows in g_tails]
        total = product(ga_ref[HAL * HAL:].reshape(PIX, -1), gb_ref[HAL * HAL:].reshape(PIX, -1), tails)
        ds_ref[...] = total if first else total + ds_in[...]


def weight_sums(idx, xa, xb, b_col, ga, gb, tails=None, partial=None):
    first = partial is None
    g_spec = pl.BlockSpec((GROUPS, GRP, CH), lambda s, m: (0, 0, 0))
    dw_spec = pl.BlockSpec((None, None, None, HALF, CH), lambda s, m: (0, jnp.minimum(s, 8) // 3, jnp.minimum(s, 8) % 3, 0, 0))
    ds_spec = pl.BlockSpec((None, HALF, CH), lambda s, m: (0, 0, 0))
    x_rows = MAIN if first else PIX
    in_specs = [pl.BlockSpec((2, x_rows, CHUNK), lambda s, m: (0, 0, 0)), pl.BlockSpec((2, x_rows, CHUNK), lambda s, m: (b_col, 0, 0)), g_spec, g_spec]
    args = [xa, xb, ga, gb]
    if not first:
        x_own, x_near, g_own, g_near = tails
        in_specs += [pl.BlockSpec((2, GRP, CHUNK), lambda s, m: (0, MAIN // GRP, 0))] * 2
        args += [x_own, x_near]
        for g in (g_own, g_near):
            for row in range(3):
                in_specs.append(pl.BlockSpec((3, GRP, CH), lambda s, m, row=row: (20 + 3 * row, 0, 0)))
            in_specs.append(pl.BlockSpec((1, GRP, CH), lambda s, m: (GROUPS - 1, 0, 0)))
            args += [g] * 4
        in_specs += [dw_spec, ds_spec]
        args += list(partial)
    return pl.pallas_call(
        functools.partial(dw_kernel, first),
        grid_spec=pltpu.PrefetchScalarGridSpec(
            num_scalar_prefetch=1,
            grid=(10,),
            in_specs=in_specs,
            out_specs=[dw_spec, ds_spec],
            scratch_shapes=[pltpu.VMEM((HALF, 2 * MAIN if first else 2 * PIX + 2 * GRP), BF16)],
        ),
        out_shape=[jax.ShapeDtypeStruct((1, 3, 3, HALF, CH), F32), jax.ShapeDtypeStruct((1, HALF, CH), F32)],
        input_output_aliases={} if first else {15: 0, 16: 1},
        compiler_params=params(1),
        cost_estimate=cost(2 * FWD_FLOPS, 2 * W_BYTES),
        name="weight_sums",
    )(idx, *args)


def solution(mesh):
    act_spec = P("stage", ("dp", "tp"), None, None, None)
    kernel_spec = P("stage", None, None, "tp", None)
    short_spec = P("stage", "tp", None)
    vec_spec = P("stage", "tp")
    grad_spec = P("stage", "dp", None, None, "tp")
    swap = [(0, 1), (1, 0)]

    def block(act_in, w_conv, w_short, gamma, beta, gamma_s, grad_z):
        idx = jnp.stack([lax.axis_index("tp"), lax.axis_index("stage")]).astype(jnp.int32)
        w_own = w_conv.reshape(9, HALF, CH)
        s_own = w_short.reshape(HALF, CH)
        x_own, x_near, img_far, w_peer, s_peer, vec, z, dzm, g = front(act_in, grad_z, gamma, beta, gamma_s, w_own, s_own)
        x_far = lax.ppermute(img_far, "stage", [(0, 1)])
        dzm_far = lax.ppermute(dzm, "dp", swap)
        g_near = lax.ppermute(g, "tp", swap)
        z_near = lax.ppermute(z, "tp", swap)
        dx_own = lax.ppermute(dx_half(g, w_own, s_own), "stage", [(1, 0)])
        dx_peer = lax.ppermute(dx_half(g, w_peer, s_peer), "stage", [(1, 0)])
        x_diag = lax.ppermute(x_far, "tp", swap)
        g_far = grads(dzm_far, vec)
        g_diag = lax.ppermute(g_far, "tp", swap)

        partial = weight_sums(idx, x_own, x_near, 0, g, g_near)
        z_out, grad_act = from_blocks(idx, z, z_near, dx_own, dx_peer)
        dw, ds = weight_sums(idx, x_far, x_diag, 1, g_far, g_diag, (x_own, x_near, g, g_near), partial)
        return z_out, grad_act, dw, ds

    return jax.shard_map(block, mesh=mesh, in_specs=(act_spec, kernel_spec, short_spec, vec_spec, vec_spec, vec_spec, grad_spec), out_specs=(grad_spec, act_spec, kernel_spec, short_spec), check_vma=False)
```

time: 258 us -> 222 us (0.86); the launches traced: 254 us -> 221 us
  waiting for transfers between devices: 96.8 us -> 53.8 us
  Pallas kernels: 129 us -> 141 us
    ppermute x9 -> x1, waiting for transfers between devices: 46.2 us -> 0.01 us  [block(): x_far = lax.ppermute(img_far, 'stage', [(0, 1)])]
    pallas_call x6 -> x3, Pallas kernels: 93.1 us -> 106 us  [the longest x2 56.5 us: weight_sums(): pl.pallas_call(functools.partial(dw_kernel, first), grid_spec=pltpu.Prefe...]
    ppermute x9 -> x1, starting transfers between devices: 5.29 us -> 1.42 us  [block(): x_far = lax.ppermute(img_far, 'stage', [(0, 1)])]
    ppermute x1, waiting for transfers between devices: 0.01 us -> 3.63 us  [block(): dx_own = lax.ppermute(dx_half(g, w_own, s_own), 'stage', [(1, 0)])]
    ppermute x1, starting transfers between devices: 2.36 us -> 5.28 us  [block(): dx_peer = lax.ppermute(dx_half(g, w_peer, s_peer), 'stage', [(1, 0)])]
    unnamed x26 -> x8, local copies, waits for them, and re-layouts: 10.4 us -> 9.66 us
  transfers between devices with their start and end apart: 16 -> 8, of which waited for: 7 -> 3; matrix products, arithmetic and copies ran while one was open for 3% -> 2% of each run, Pallas kernels for 33% -> 28%
where the time goes in v2:
time: 222 us; the launch traced here: 221 us
  Pallas kernels  141 us (64%)
  waiting for transfers between devices  53.8 us (24%)
  starting transfers between devices  14.9 us (7%)
  local copies, waits for them, and re-layouts  9.66 us (4%)
    pallas_call x2, Pallas kernels, weight_sums(): pl.pallas_call(functools.partial(dw_kernel, first), grid_spec=pltpu.Prefe...  56.5 us
    pallas_call x1, Pallas kernels, front(): pl.pallas_call(front_kernel, in_specs=[vmem] * 5 + [anywhere] * 2, out_sp...  49.1 us
    ppermute x1, waiting for transfers between devices, block(): dzm_far = lax.ppermute(dzm, 'dp', swap)  34.6 us
    pallas_call x2, Pallas kernels, dx_half(): pl.pallas_call(dx_kernel, grid=(HALF // TILE,), in_specs=[pl.BlockSpec((G...  26.5 us
    ppermute x1, waiting for transfers between devices, block(): dx_peer = lax.ppermute(dx_half(g, w_peer, s_peer), 'stage', [(1, 0)])  15.5 us
    unnamed x8, local copies, waits for them, and re-layouts  9.66 us
    ppermute x1, starting transfers between devices, block(): dx_own = lax.ppermute(dx_half(g, w_own, s_own), 'stage', [(1, 0)])  6.65 us
    ppermute x1, starting transfers between devices, block(): dx_peer = lax.ppermute(dx_half(g, w_peer, s_peer), 'stage', [(1, 0)])  5.28 us
  transfers between devices with their start and end apart: 8, of which 3 were waited for; matrix products, arithmetic and copies ran while one was open for 2% of the time, Pallas kernels for 28%

profile of v2, /device:TPU:2, one launch (start us, length us, event | category | flops | bytes accessed | tf_op | source)
XLA Modules:
  0.0 221.0 jit_solution(10346146448516163614)
XLA Ops:
  0.6 3.0 %copy.13.grad = bf16[1,2,28,28,512]{4,3,2,1,0:T(8,128)(2,1)} copy(bf16[1,2,28,28,512]{4,1,3,2,0:T(2,128)(2,1)} %param.13) | data formatting | bytes 3211264 | tf_op args[6]
  3.7 49.1 %front.1 = (bf16[2,784,256]{2,1,0:T(8,128)(2,1)}, bf16[2,784,256]{2,1,0:T(8,128)(2,1)}, bf16[4,784,256]{2,1,0:T(8,128)(2,1)}, bf16[9,512,1024]{2,1,0:T(8,128)(2,...) custom-call(bf16[1,1,28,28,1024]{4,3,2,1,0:T(8,128)(2,1)} %act.1, ...), custom_call_target="tpu_custom_call" | custom-call | flops 16441671680 | bytes 20971520 | tf_op jit(solution)/shard_map/front/pallas_call | solution.py:339
  52.8 1.5 collective-permute-start.5
  54.3 0.0 collective-permute-start.7
  54.3 34.6 %collective-permute-done.5.dzm_ref = bf16[784,1024]{1,0:T(8,128)(2,1)S(1)} collective-permute-done((bf16[784,1024]{1,0:T(8,128)(2,1)}, bf16[784,1024]{1,0:T(8,128)(2,1)S(1)}, u32[]{:S(2)}, u32[]{:S(2)}) %collective-permute-start.5) | collective-permute-done | bytes 1605664 | tf_op jit(solution)/shard_map/ppermute | solution.py:514
  89.0 0.0 copy-start.2
  89.0 1.2 copy-done.2
  90.1 4.4 %grads.1.refs_2_ = bf16[130,16,1024]{2,1,0:T(8,128)(2,1)} custom-call(bf16[784,1024]{1,0:T(8,128)(2,1)} %copy-done.2, f32[3,1024]{1,0:T(4,128)} %get-tuple-element.27.vec_ref), custom_call_target="tpu_custom_call" | custom-call | flops 6422528 | bytes 6422528 | tf_op jit(solution)/shard_map/grads/pallas_call | solution.py:155
  94.6 0.0 collective-permute-start.6
  94.6 0.0 copy-start
  94.6 1.4 collective-permute-start.3
  96.0 13.3 %dx_half.2 = bf16[784,512]{1,0:T(8,128)(2,1)} custom-call(bf16[130,16,1024]{2,1,0:T(8,128)(2,1)} %get-tuple-element.20.gh_ref.refs_2_.refs_6_.refs_7_.refs_8_.refs_9_, bf16[9,512,1024]{2,1,0:T(8,128)(2,1)} %bitcast.5, bf16[512,1024]{1,0:T(8,128)(2,1)} %bitcast.7), custom_call_target="tpu_custom_call" | custom-call | flops 8220835840 | bytes 10485760 | tf_op jit(solution)/shard_map/dx_half/pallas_call | solution.py:394
  109.3 6.6 %collective-permute-start.1 = (bf16[784,512]{1,0:T(8,128)(2,1)}, bf16[784,512]{1,0:T(8,128)(2,1)}, u32[]{:S(2)}, u32[]{:S(2)}) collective-permute-start(bf16[784,512]{1,0:T(8,128)(2,1)} %dx_half.2), channel_id=1, source_target_pairs={{2,0},{3,1},{6,4},{7,5}} | collective-permute-start | bytes 2408456 | tf_op jit(solution)/shard_map/ppermute | solution.py:517
  115.9 0.0 copy-done
  115.9 0.0 collective-permute-start
  115.9 13.3 %dx_half.3 = bf16[784,512]{1,0:T(8,128)(2,1)} custom-call(bf16[130,16,1024]{2,1,0:T(8,128)(2,1)} %get-tuple-element.20.gh_ref.refs_2_.refs_6_.refs_7_.refs_8_.refs_9_, bf16[9,512,1024]{2,1,0:T(8,128)(2,1)} %get-tuple-element.21.w_ref, bf16[512,1024]{1,0:T(8,128)(2,1)} %get-tuple-element.22.s_ref), custom_call_target="tpu_custom_call" | custom-call | flops 8220835840 | bytes 10485760 | tf_op jit(solution)/shard_map/dx_half/pallas_call | solution.py:394
  129.2 3.6 %collective-permute-done.1.dx_own_ref = bf16[784,512]{1,0:T(8,128)(2,1)} collective-permute-done((bf16[784,512]{1,0:T(8,128)(2,1)}, bf16[784,512]{1,0:T(8,128)(2,1)}, u32[]{:S(2)}, u32[]{:S(2)}) %collective-permute-start.1) | collective-permute-done | bytes 802848 | tf_op jit(solution)/shard_map/ppermute | solution.py:517
  132.8 5.3 %collective-permute-start.2 = (bf16[784,512]{1,0:T(8,128)(2,1)}, bf16[784,512]{1,0:T(8,128)(2,1)}, u32[]{:S(2)}, u32[]{:S(2)}) collective-permute-start(bf16[784,512]{1,0:T(8,128)(2,1)} %dx_half.3), channel_id=1, source_target_pairs={{2,0},{3,1},{6,4},{7,5}} | collective-permute-start | bytes 2408456 | tf_op jit(solution)/shard_map/ppermute | solution.py:518
  138.1 0.0 collective-permute-done.3.refs_0_
  138.1 0.0 collective-permute-start.4
  138.1 0.6 pad_add_fusion.idx_ref
  138.7 15.5 %collective-permute-done.2.dx_peer_ref = bf16[784,512]{1,0:T(8,128)(2,1)} collective-permute-done((bf16[784,512]{1,0:T(8,128)(2,1)}, bf16[784,512]{1,0:T(8,128)(2,1)}, u32[]{:S(2)}, u32[]{:S(2)}) %collective-permute-start.2) | collective-permute-done | bytes 802848 | tf_op jit(solution)/shard_map/ppermute | solution.py:518
  154.2 0.0 collective-permute-done.z_near_ref
  154.2 0.0 copy-start.1
  154.2 1.2 copy-done.1
  155.3 4.8 %from_blocks.1 = (bf16[1,2,28,28,512]{4,3,2,1,0:T(8,128)(2,1)}, bf16[1,1,28,28,1024]{4,3,2,1,0:T(8,128)(2,1)}) custom-call(s32[2]{0:T(128)} %pad_add_fusion.idx_ref, bf16[784,1024]{1,0:T(8,128)(2,1)} %get-tuple-element.19.z_ref, bf16[784,1024]{1,0:T(8,128)(2,1)} %copy-done.1, bf16[784,512]{1,0:T(8,128)(2,1)} %collective-permute-done.1.dx_own_ref, ...), custom_call_target="tpu_custom_call" | custom-call | flops 411041792 | bytes 6422528 | tf_op jit(solution)/shard_map/from_blocks/pallas_call | solution.py:78
  160.2 4.3 %copy.14 = bf16[1,2,28,28,512]{4,1,3,2,0:T(2,128)(2,1)} copy(bf16[1,2,28,28,512]{4,3,2,1,0:T(8,128)(2,1)} %get-tuple-element.34) | data formatting | bytes 3211264
  164.5 0.0 collective-permute-done.7.refs_3_.refs_10_.refs_11_.refs_12_.refs_13_
  164.5 25.8 %weight_sums.2 = (f32[1,3,3,512,1024]{4,3,2,1,0:T(8,128)}, f32[1,512,1024]{2,1,0:T(8,128)}) custom-call(s32[2]{0:T(128)} %pad_add_fusion.idx_ref, bf16[2,784,256]{2,1,0:T(8,128)(2,1)} %get-tuple-element.28.refs_0_.refs_4_, bf16[2,784,256]{2,1,0:T(8,128)(2,1)} %get-tuple-element.29.refs_1_.refs_5_, ...), custom_call_target="tpu_custom_call" | custom-call | flops 16441671680 | bytes 20971520 | tf_op jit(solution)/shard_map/weight_sums/pallas_call | solution.py:483
  190.3 0.0 collective-permute-done.4.refs_1_
  190.3 0.0 collective-permute-done.6.refs_3_
  190.3 30.7 %weight_sums.3 = (f32[1,3,3,512,1024]{4,3,2,1,0:T(8,128)}, f32[1,512,1024]{2,1,0:T(8,128)}) custom-call(s32[2]{0:T(128)} %pad_add_fusion.idx_ref, bf16[4,784,256]{2,1,0:T(8,128)(2,1)} %collective-permute-done.3.refs_0_, bf16[4,784,256]{2,1,0:T(8,128)(2,1)} %collective-permute-done.4.refs_1_, ...), custom_call_target="tpu_custom_call", output_to_operand_aliasing={{0}: (15, {}), {1}: (16, {})} | custom-call | flops 16441671680 | bytes 20971520 | tf_op jit(solution)/shard_map/weight_sums/pallas_call | solution.py:483
Async XLA Ops:
  52.8 36.2 %collective-permute-start.5 = (bf16[784,1024]{1,0:T(8,128)(2,1)}, bf16[784,1024]{1,0:T(8,128)(2,1)S(1)}, u32[]{:S(2)}, u32[]{:S(2)}) collective-permute-start(bf16[784,1024]{1,0:T(8,128)(2,1)} %get-tuple-element.26), channel_id=1, source_target_pairs={{0,4},{4,0},{1,5},{5,1},{2,6},{6,2},{3,7},{7,3}} | collective-permute-start | bytes 4816904 | tf_op jit(solution)/shard_map/ppermute | solution.py:514
  54.3 110.2 %collective-permute-start.7 = (bf16[130,16,1024]{2,1,0:T(8,128)(2,1)}, bf16[130,16,1024]{2,1,0:T(8,128)(2,1)}, u32[]{:S(2)}, u32[]{:S(2)}) collective-permute-start(bf16[130,16,1024]{2,1,0:T(8,128)(2,1)} %get-tuple-element.20.gh_ref.refs_2_.refs_6_.refs_7_.refs_8_.refs_9_), channel_id=1, source_target_pairs={{0,1},{1,0},{2,3},{3,2},{4,5},{5,4},{6,7},{7,6}} | collective-permute-start | bytes 12779528 | tf_op jit(solution)/shard_map/ppermute | solution.py:515
  89.0 1.2 copy-start.2
  94.6 95.8 %collective-permute-start.6 = (bf16[130,16,1024]{2,1,0:T(8,128)(2,1)}, bf16[130,16,1024]{2,1,0:T(8,128)(2,1)}, u32[]{:S(2)}, u32[]{:S(2)}) collective-permute-start(bf16[130,16,1024]{2,1,0:T(8,128)(2,1)} %grads.1.refs_2_), channel_id=1, source_target_pairs={{0,1},{1,0},{2,3},{3,2},{4,5},{5,4},{6,7},{7,6}} | collective-permute-start | bytes 12779528 | tf_op jit(solution)/shard_map/ppermute | solution.py:521
  94.6 21.3 %copy-start = (bf16[784,1024]{1,0:T(8,128)(2,1)S(1)}, bf16[784,1024]{1,0:T(8,128)(2,1)}, u32[]{:S(2)}) copy-start(bf16[784,1024]{1,0:T(8,128)(2,1)} %get-tuple-element.19.z_ref) | copy-start | bytes 4816900
  94.6 43.5 %collective-permute-start.3 = (bf16[4,784,256]{2,1,0:T(8,128)(2,1)}, bf16[4,784,256]{2,1,0:T(8,128)(2,1)}, u32[]{:S(2)}, u32[]{:S(2)}) collective-permute-start(bf16[4,784,256]{2,1,0:T(8,128)(2,1)} %get-tuple-element.25), channel_id=1, source_target_pairs={{0,2},{1,3},{4,6},{5,7}} | collective-permute-start | bytes 4816904 | tf_op jit(solution)/shard_map/ppermute | solution.py:513
  109.3 23.5 %collective-permute-start.1 = (bf16[784,512]{1,0:T(8,128)(2,1)}, bf16[784,512]{1,0:T(8,128)(2,1)}, u32[]{:S(2)}, u32[]{:S(2)}) collective-permute-start(bf16[784,512]{1,0:T(8,128)(2,1)} %dx_half.2), channel_id=1, source_target_pairs={{2,0},{3,1},{6,4},{7,5}} | collective-permute-start | bytes 2408456 | tf_op jit(solution)/shard_map/ppermute | solution.py:517
  115.9 38.3 %collective-permute-start = (bf16[784,1024]{1,0:T(8,128)(2,1)S(1)}, bf16[784,1024]{1,0:T(8,128)(2,1)S(1)}, u32[]{:S(2)}, u32[]{:S(2)}) collective-permute-start(bf16[784,1024]{1,0:T(8,128)(2,1)S(1)} %copy-done), channel_id=1, source_target_pairs={{0,1},{1,0},{2,3},{3,2},{4,5},{5,4},{6,7},{7,6}} | collective-permute-start | bytes 4816904 | tf_op jit(solution)/shard_map/ppermute | solution.py:516
  132.8 21.4 %collective-permute-start.2 = (bf16[784,512]{1,0:T(8,128)(2,1)}, bf16[784,512]{1,0:T(8,128)(2,1)}, u32[]{:S(2)}, u32[]{:S(2)}) collective-permute-start(bf16[784,512]{1,0:T(8,128)(2,1)} %dx_half.3), channel_id=1, source_target_pairs={{2,0},{3,1},{6,4},{7,5}} | collective-permute-start | bytes 2408456 | tf_op jit(solution)/shard_map/ppermute | solution.py:518
  138.1 52.2 %collective-permute-start.4 = (bf16[4,784,256]{2,1,0:T(8,128)(2,1)}, bf16[4,784,256]{2,1,0:T(8,128)(2,1)}, u32[]{:S(2)}, u32[]{:S(2)}) collective-permute-start(bf16[4,784,256]{2,1,0:T(8,128)(2,1)} %collective-permute-done.3.refs_0_), channel_id=1, source_target_pairs={{0,1},{1,0},{2,3},{3,2},{4,5},{5,4},{6,7},{7,6}} | collective-permute-start | bytes 4816904 | tf_op jit(solution)/shard_map/ppermute | solution.py:519
  154.2 1.2 copy-start.1

commit v3 on v2

v3 whole, which is shorter than its diff:
```python
import jax
import jax.numpy as jnp
from jax import lax
from jax.experimental import pallas as pl
from jax.experimental.pallas import tpu as pltpu
from jax.sharding import PartitionSpec as P

SIDE = 28
LO = 7
GRP = 16
HAL = LO + 2
GROUPS = HAL * HAL + LO * LO
PIX = SIDE * SIDE
HALF = 512
CH = 1024
TILE = 256
CHUNK = 256
N_CHUNKS = CH // CHUNK
MAIN = 768
MESH = pl.DeviceIdType.MESH
F32 = jnp.float32
BF16 = jnp.bfloat16
VMEM_LIMIT = 60 * 1024 * 1024


def params(n_axes):
    return pltpu.CompilerParams(dimension_semantics=("arbitrary",) * n_axes, vmem_limit_bytes=VMEM_LIMIT)


def cost(flops, bytes_accessed):
    return pl.CostEstimate(flops=int(flops), bytes_accessed=int(bytes_accessed), transcendentals=0)


def order_matrix(transposed):
    shape = (128, 112) if transposed else (112, 128)
    row = lax.broadcasted_iota(jnp.int32, shape, 1 if transposed else 0)
    col = lax.broadcasted_iota(jnp.int32, shape, 0 if transposed else 1)
    w_lo, h_hi, w_hi = row // 16, (row // 4) % 4, row % 4
    return (col == h_hi * 32 + w_hi * 7 + w_lo).astype(F32).astype(BF16)


def pair_matrix(first, transposed):
    shape = (224, 224) if transposed else (112, 224)
    row = lax.broadcasted_iota(jnp.int32, shape, 1 if transposed else 0)
    col = lax.broadcasted_iota(jnp.int32, shape, 0 if transposed else 1)
    image = (row // 112 + first) % 2
    row = row % 112
    w_lo, h_hi, w_hi = row // 16, (row // 4) % 4, row % 4
    return (col == h_hi * 56 + (w_hi * 7 + w_lo) * 2 + image).astype(F32).astype(BF16)


def from_blocks_kernel(idx_ref, z_ref, z_near_ref, dx_ref, z_out, dx_out):
    stage = idx_ref[1]

    @pl.when(stage == 0)
    def _():
        z_out[...] = jnp.zeros_like(z_out)
        select = order_matrix(True)
        for lo in range(LO):
            for q in range(2):
                rows = jnp.dot(select, dx_ref[q, lo * 112:(lo + 1) * 112, :], preferred_element_type=F32).astype(BF16)
                for hi in range(4):
                    dx_out[hi * LO + lo, :, q * CHUNK:(q + 1) * CHUNK] = rows[hi * 32:hi * 32 + SIDE, :]

    @pl.when(stage == 1)
    def _():
        dx_out[...] = jnp.zeros_like(dx_out)
        select = pair_matrix(idx_ref[0], True)
        for lo in range(LO):
            part = slice(lo * 112, (lo + 1) * 112)
            both = jnp.concatenate([z_ref[part, :], z_near_ref[part, :]], axis=0)
            rows = jnp.dot(select, both, preferred_element_type=F32)
            for hi in range(4):
                z_out[hi * LO + lo] = rows[hi * 56:(hi + 1) * 56].astype(BF16).reshape(SIDE, 2, CHUNK)


def from_blocks(idx, z, z_near, dx):
    z_out, dx_out = pl.pallas_call(
        from_blocks_kernel,
        grid_spec=pltpu.PrefetchScalarGridSpec(
            num_scalar_prefetch=1,
            grid=(2,),
            in_specs=[
                pl.BlockSpec((PIX, CHUNK), lambda k, m: (0, k)),
                pl.BlockSpec((PIX, CHUNK), lambda k, m: (0, k)),
                pl.BlockSpec((2, PIX, CHUNK), lambda k, m: (k, 0, 0)),
            ],
            out_specs=[
                pl.BlockSpec((SIDE, SIDE, 2, CHUNK), lambda k, m: (0, 0, 0, k)),
                pl.BlockSpec((None, None, SIDE, SIDE, HALF), lambda k, m: (0, 0, 0, 0, (m[0] + k) % 2)),
            ],
        ),
        out_shape=[
            jax.ShapeDtypeStruct((SIDE, SIDE, 2, HALF), BF16),
            jax.ShapeDtypeStruct((1, 1, SIDE, SIDE, CH), BF16),
        ],
        compiler_params=params(1),
        cost_estimate=cost(2 * 2 * 7 * 112 * 128 * HALF * 2, 4 * 2 * PIX * HALF * 2),
        name="from_blocks",
    )(idx, z, z_near, dx)
    return jnp.transpose(z_out, (2, 0, 1, 3))[None], dx_out


def moved(tile, step_h, step_w):
    wide = tile.astype(F32)
    n = wide.shape[1]
    if step_h < 0:
        wide = jnp.concatenate([jnp.zeros((4, n), F32), wide[:12]], axis=0)
    if step_h > 0:
        wide = jnp.concatenate([wide[4:], jnp.zeros((4, n), F32)], axis=0)
    if step_w:
        w_hi = lax.broadcasted_iota(jnp.int32, (GRP, n), 0) % 4
        if step_w < 0:
            wide = jnp.concatenate([wide[15:], wide[:15]], axis=0)
            wide = jnp.where(w_hi == 0, 0.0, wide)
        else:
            wide = jnp.concatenate([wide[1:], wide[:1]], axis=0)
            wide = jnp.where(w_hi == 3, 0.0, wide)
    return wide.astype(BF16)


def fill_halo(dst_ref, value):
    n = value.shape[1]
    groups = value.reshape(LO, LO, GRP, n)
    for a in range(HAL):
        step_h = -1 if a == 0 else (1 if a == HAL - 1 else 0)
        if not step_h:
            dst_ref[a * HAL + 1:a * HAL + 1 + LO] = groups[a - 1]
        for b in range(HAL):
            step_w = -1 if b == 0 else (1 if b == HAL - 1 else 0)
            if step_h or step_w:
                dst_ref[a * HAL + b] = moved(groups[(a - 1) % LO, (b - 1) % LO], step_h, step_w)


def window(ref, i, j):
    parts = [ref[pl.ds((i + a) * HAL + j, LO)] for a in range(LO)]
    whole = jnp.concatenate(parts, axis=0)
    return whole.reshape(PIX, whole.shape[-1])


def both_grads(dz, vec_ref, g_ref):
    g_ref[HAL * HAL:] = (dz * vec_ref[2:3, :]).astype(BF16).reshape(LO * LO, GRP, -1)
    fill_halo(g_ref, (dz * vec_ref[0:1, :]).astype(BF16))


FWD_FLOPS = 2 * PIX * HALF * CH * 10
W_BYTES = 10 * HALF * CH * 2


def dot_nt(a, b):
    return lax.dot_general(a, b, (((1,), (1,)), ((), ())), preferred_element_type=F32)


def tap_rows(ref, tap):
    last = tap // 9
    base = (1 - last) * ((2 - tap // 3) * HAL + 2 - tap % 3) + last * HAL * HAL
    pitch = HAL - 2 * last
    parts = [ref[pl.ds(base + a * pitch, LO if a < LO - 1 else LO - 1)] for a in range(LO)]
    return jnp.concatenate(parts, axis=0).reshape(MAIN, CH)


def main_kernel(
    act, grad, gam, bet, gms, w_own, s_own,
    x_far, x_diag, x_tails, w_peer, s_peer, vec_out, z_out, z_near, dzm_far, dzm_diag, g_tails, dx_in, sums,
    act_in, pad, xs, xr, xn, xh, im, w_buf, s_buf, pre, short, grad_in, dz_own, dz_send, dz_peer, vec_peer, z_st, dzm_st, g_st, g_near,
    act_sem, x_sem, far_sem, hop_sem, near_sem, diag_sem, w_sem, vec_sem, peer_sem, dzm_sem, dx_sem, w_local, keep_sem, tail_sem, out_sem, sum_sem,
):
    t = lax.axis_index("tp")
    stage = lax.axis_index("stage")
    dp = lax.axis_index("dp")

    def act_copy(q):
        col = pl.multiple_of(lax.rem(t * HALF + q * CHUNK, CH), CHUNK)
        return pltpu.make_async_copy(act.at[0, 0, :, :, pl.ds(col, CHUNK)], act_in.at[q], act_sem.at[q])

    grad_copy = pltpu.make_async_copy(grad, grad_in, act_sem.at[4])

    def w_fetch(src_w, src_s, block, q):
        rows = pl.ds(block * CHUNK, CHUNK)
        return (
            pltpu.make_async_copy(src_w.at[:, rows], w_buf.at[q], w_local.at[q, 0]),
            pltpu.make_async_copy(src_s.at[rows], s_buf.at[q], w_local.at[q, 1]),
        )

    @pl.when(stage == 0)
    def _():
        for q in range(N_CHUNKS):
            act_copy(q).start()

    @pl.when(stage == 1)
    def _():
        grad_copy.start()
        for q in range(2):
            for copy in w_fetch(w_own, s_own, q, q):
                copy.start()

    barrier = pltpu.get_barrier_semaphore()
    for target in ({"tp": 1 - t}, {"stage": 1 - stage}, {"dp": 1 - dp}):
        pl.semaphore_signal(barrier, inc=1, device_id=target, device_id_type=MESH)
    pl.semaphore_wait(barrier, 3)

    def remote(src, dst, sems, target):
        return pltpu.make_async_remote_copy(src_ref=src, dst_ref=dst, send_sem=sems.at[0], recv_sem=sems.at[1], device_id=target, device_id_type=MESH)

    peer, other_stage, other_dp = {"tp": 1 - t}, {"stage": 1 - stage}, {"dp": 1 - dp}

    def x_copy(q):
        return remote(xs.at[q], xr.at[q], x_sem.at[q], other_stage)

    def far_copy(q):
        return remote(xs.at[q], xr.at[q], far_sem.at[q], other_dp)

    def hop_copy(q):
        return remote(xr.at[q], x_far.at[q], hop_sem.at[q], other_stage)

    def dx_copy(q):
        return remote(xs.at[q], dx_in.at[q], dx_sem.at[q], other_stage)

    @pl.when(stage == 0)
    def _():
        pad[...] = jnp.zeros_like(pad)
        select = order_matrix(False)
        for q in range(N_CHUNKS):
            act_copy(q).wait()
            pad[:, :SIDE, :] = act_in[q]
            for lo in range(LO):
                rows = jnp.concatenate([pad[hi * LO + lo] for hi in range(4)], axis=0)
                xs[q, lo * 112:(lo + 1) * 112, :] = jnp.dot(select, rows, preferred_element_type=F32).astype(BF16)
            x_copy(q).start()
            far_copy(q).start()
        for q in range(N_CHUNKS):
            far_copy(q).wait_recv()
            hop_copy(q).start()
        for q in range(N_CHUNKS):
            x_copy(q).wait_send()
            far_copy(q).wait_send()
            hop_copy(q).wait_send()
            dx_copy(q).wait_recv()

    @pl.when(stage == 1)
    def _():
        w_copy = remote(w_own, w_peer, w_sem.at[0], peer)
        s_copy = remote(s_own, s_peer, w_sem.at[1], peer)
        vec_copies = [remote(ref, vec_peer.at[k], vec_sem.at[k], peer) for k, ref in enumerate((gam, bet, gms))]
        w_copy.start()
        s_copy.start()
        for copy in vec_copies:
            copy.start()

        grad_copy.wait()
        for image, dst in ((1 - t, dz_send), (t, dz_own)):
            select = pair_matrix(image, False)
            for lo in range(LO):
                rows = jnp.concatenate([grad_in[hi * LO + lo].reshape(56, HALF) for hi in range(4)], axis=0)
                dst[lo * 112:(lo + 1) * 112, :] = jnp.dot(select, rows, preferred_element_type=F32).astype(BF16)
        dz_copy = remote(dz_send, dz_peer, peer_sem.at[0], peer)
        dz_copy.start()

        def near_copy(q):
            return remote(xr.at[q], xn.at[q - 2], near_sem.at[q - 2], peer)

        def chunk(q, carry):
            x_copy(q).wait_recv()

            @pl.when(q >= 2)
            def _():
                near_copy(q).start()

            fill_halo(xh, xr[q])
            for i in range(3):
                for j in range(3):
                    k = i * 3 + j
                    im[:, k * CHUNK:(k + 1) * CHUNK] = window(xh, i, j)

            @pl.when(q == 1)
            def _():
                w_copy.wait_recv()
                s_copy.wait_recv()
                for k in range(2):
                    for copy in w_fetch(w_peer, s_peer, k, k + 2):
                        copy.start()

            for copy in w_fetch(w_own, s_own, 0, q):
                copy.wait()
            for n in range(2):
                cols = slice(n * HALF, (n + 1) * HALF)
                main = jnp.dot(im[...], w_buf[q, :, :, cols].reshape(9 * CHUNK, HALF), preferred_element_type=F32)
                side = jnp.dot(xr[q], s_buf[q, :, cols], preferred_element_type=F32)

                @pl.when(q == 0)
                def _():
                    pre[:, cols] = main
                    short[:, cols] = side

                @pl.when(q > 0)
                def _():
                    pre[:, cols] += main
                    short[:, cols] += side

            return carry

        lax.fori_loop(0, N_CHUNKS, chunk, 0)

        for copy in vec_copies:
            copy.wait_recv()
        dz_copy.wait_recv()
        for n in range(CH // TILE):
            half, part = n // 2, slice((n % 2) * TILE, (n % 2 + 1) * TILE)
            cols = slice(n * TILE, (n + 1) * TILE)
            mine = t == half
            gamma, beta, gamma_s = (jnp.where(mine, ref[:, part], vec_peer[k, :, part]) for k, ref in enumerate((gam, bet, gms)))
            for k, row in enumerate((gamma, beta, gamma_s)):
                vec_out[k:k + 1, cols] = row
            u = pre[:, cols] * gamma + beta + short[:, cols] * gamma_s
            z_st[:, cols] = jnp.maximum(u, 0.0).astype(BF16)
            dz = jnp.where(mine, dz_own[:, part].astype(F32), dz_peer[:, part].astype(F32))
            dz = jnp.where(u > 0.0, dz, 0.0)
            dzm_st[:, cols] = dz.astype(BF16)
            g_st[HAL * HAL:, :, cols] = (dz * gamma_s).astype(BF16).reshape(LO * LO, GRP, TILE)
            fill_halo(g_st.at[:, :, cols], (dz * gamma).astype(BF16))

        dzm_copy = remote(dzm_st, dzm_far, dzm_sem.at[0], other_dp)
        g_copy = remote(g_st, g_near, peer_sem.at[1], peer)
        mine_at, theirs_at = pl.multiple_of(t * HALF, HALF), pl.multiple_of((1 - t) * HALF, HALF)
        z_copy = remote(z_st.at[:, pl.ds(theirs_at, HALF)], z_near, peer_sem.at[2], peer)
        z_keep = pltpu.make_async_copy(z_st.at[:, pl.ds(mine_at, HALF)], z_out, keep_sem)
        for copy in (dzm_copy, g_copy, z_copy, z_keep):
            copy.start()

        def dx_chunk(q, carry):
            total = dot_nt(g_st[HAL * HAL:].reshape(PIX, CH), s_buf[q])
            for k in range(9):
                total = total + dot_nt(window(g_st, 2 - k // 3, 2 - k % 3), w_buf[q, k])
            xs[q] = total.astype(BF16)
            dx_copy(q).start()
            return carry

        lax.fori_loop(0, N_CHUNKS, dx_chunk, 0)

        near_copy(2).wait_recv()
        near_copy(3).wait_recv()
        g_copy.wait_recv()
        tails = []
        for k, (x_ref, g_ref) in enumerate(((xr, g_st), (xn, g_near))):
            tails.append(pltpu.make_async_copy(x_ref.at[0:2, MAIN:PIX], x_tails.at[k], tail_sem.at[k, 0]))
            for i in range(3):
                at = (LO - 1 + i) * HAL + LO - 1
                tails.append(pltpu.make_async_copy(g_ref.at[at:at + 3], g_tails.at[k, 3 * i:3 * i + 3], tail_sem.at[k, 1 + i]))
            tails.append(pltpu.make_async_copy(g_ref.at[GROUPS - 1:GROUPS], g_tails.at[k, 9:10], tail_sem.at[k, 4]))
        for copy in tails:
            copy.start()
        for q in range(2):
            rows = slice(q * CHUNK, (q + 1) * CHUNK)
            im[rows, :MAIN] = xr[q, :MAIN, :].T
            im[rows, MAIN:2 * MAIN] = xn[q, :MAIN, :].T

        def diag_copy(k):
            return remote(x_far.at[2 + k], x_diag.at[k], diag_sem.at[k], peer)

        dzm_diag_copy = remote(dzm_far, dzm_diag, dzm_sem.at[1], peer)

        def sum_copy(tap, k):
            return pltpu.make_async_copy((pre, short)[k].at[:HALF], sums.at[tap], sum_sem.at[k])

        def sum_pair(p, carry):
            @pl.when(p == 2)
            def _():
                for k in range(2):
                    hop_copy(2 + k).wait_recv()
                    diag_copy(k).start()

            @pl.when(p == 4)
            def _():
                dzm_copy.wait_recv()
                dzm_diag_copy.start()

            for k in range(2):
                tap = 2 * p + k
                rows = jnp.concatenate([tap_rows(g_st, tap), tap_rows(g_near, tap)], axis=0)
                total = jnp.dot(im[:HALF, :2 * MAIN], rows, preferred_element_type=F32)

                @pl.when(p > 0)
                def _():
                    sum_copy(tap - 2, k).wait()

                (pre, short)[k][:HALF] = total
                sum_copy(tap, k).start()
            return carry

        lax.fori_loop(0, 5, sum_pair, 0)

        for k in range(2):
            sum_copy(8 + k, k).wait()
            hop_copy(k).wait_recv()
            near_copy(2 + k).wait_send()
            diag_copy(k).wait()
        for q in range(N_CHUNKS):
            dx_copy(q).wait_send()
        for copy in tails:
            copy.wait()
        z_keep.wait()
        z_copy.wait()
        dzm_diag_copy.wait()
        for copy in [w_copy, s_copy, dz_copy, dzm_copy, g_copy] + vec_copies:
            copy.wait_send()


def main(act_in, grad_z, gamma, beta, gamma_s, w_own, s_own):
    vmem = pl.BlockSpec(memory_space=pltpu.VMEM)
    anywhere = pl.BlockSpec(memory_space=pl.ANY)
    dma = pltpu.SemaphoreType.DMA
    chunks = (N_CHUNKS, PIX, CHUNK)
    return pl.pallas_call(
        main_kernel,
        in_specs=[anywhere] * 2 + [vmem] * 3 + [anywhere] * 2,
        out_specs=[anywhere] * 5 + [vmem] + [anywhere] * 7,
        out_shape=[
            jax.ShapeDtypeStruct(chunks, BF16),
            jax.ShapeDtypeStruct((2, PIX, CHUNK), BF16),
            jax.ShapeDtypeStruct((2, 2, GRP, CHUNK), BF16),
            jax.ShapeDtypeStruct((9, HALF, CH), BF16),
            jax.ShapeDtypeStruct((HALF, CH), BF16),
            jax.ShapeDtypeStruct((3, CH), F32),
            jax.ShapeDtypeStruct((PIX, HALF), BF16),
            jax.ShapeDtypeStruct((PIX, HALF), BF16),
            jax.ShapeDtypeStruct((PIX, CH), BF16),
            jax.ShapeDtypeStruct((PIX, CH), BF16),
            jax.ShapeDtypeStruct((2, 10, GRP, CH), BF16),
            jax.ShapeDtypeStruct(chunks, BF16),
            jax.ShapeDtypeStruct((10, HALF, CH), F32),
        ],
        scratch_shapes=[
            pltpu.VMEM((N_CHUNKS, SIDE, SIDE, CHUNK), BF16),
            pltpu.VMEM((SIDE, 32, CHUNK), BF16),
            pltpu.VMEM(chunks, BF16),
            pltpu.VMEM(chunks, BF16),
            pltpu.VMEM((2, PIX, CHUNK), BF16),
            pltpu.VMEM((HAL * HAL, GRP, CHUNK), BF16),
            pltpu.VMEM((PIX, 9 * CHUNK), BF16),
            pltpu.VMEM((N_CHUNKS, 9, CHUNK, CH), BF16),
            pltpu.VMEM((N_CHUNKS, CHUNK, CH), BF16),
            pltpu.VMEM((PIX, CH), F32),
            pltpu.VMEM((PIX, CH), F32),
            pltpu.VMEM((SIDE, SIDE, 2, HALF), BF16),
            pltpu.VMEM((PIX, HALF), BF16),
            pltpu.VMEM((PIX, HALF), BF16),
            pltpu.VMEM((PIX, HALF), BF16),
            pltpu.VMEM((3, 1, HALF), F32),
            pltpu.VMEM((PIX, CH), BF16),
            pltpu.VMEM((PIX, CH), BF16),
            pltpu.VMEM((GROUPS, GRP, CH), BF16),
            pltpu.VMEM((GROUPS, GRP, CH), BF16),
            dma((5,)), dma((4, 2)), dma((4, 2)), dma((4, 2)), dma((2, 2)), dma((2, 2)), dma((2, 2)), dma((3, 2)), dma((3, 2)), dma((2, 2)),
            dma((4, 2)), dma((4, 2)), dma, dma((2, 5)), dma, dma((2,)),
        ],
        compiler_params=pltpu.CompilerParams(collective_id=0, has_side_effects=True, vmem_limit_bytes=66 * 1000 * 1000),
        cost_estimate=cost(6 * FWD_FLOPS, 2 * W_BYTES),
        name="main",
    )(act_in, jnp.transpose(grad_z[0], (1, 2, 0, 3)), gamma, beta, gamma_s, w_own, s_own)


def last_kernel(idx_ref, xa_ref, xb_ref, x_tails, dza_ref, dzb_ref, vec_ref, g_tails, dw_in, dw_ref, ds_ref, ga_ref, gb_ref, xt_ref):
    step = pl.program_id(0)
    stage = idx_ref[1]

    @pl.when((step == 0) & (stage == 1))
    def _():
        for q in range(2):
            rows = slice(q * CHUNK, (q + 1) * CHUNK)
            xt_ref[rows, :MAIN] = xa_ref[q, :MAIN, :].T
            xt_ref[rows, MAIN:2 * MAIN] = xb_ref[q, :MAIN, :].T
            ends = [xa_ref[q, MAIN:, :], xb_ref[q, MAIN:, :], x_tails[0, q], x_tails[1, q]]
            xt_ref[rows, 2 * MAIN:] = jnp.concatenate(ends, axis=0).T
        for dz_ref, g_ref in ((dza_ref, ga_ref), (dzb_ref, gb_ref)):
            for n in range(CH // TILE):
                cols = slice(n * TILE, (n + 1) * TILE)
                both_grads(dz_ref[:, cols].astype(F32), vec_ref.at[:, cols], g_ref.at[:, :, cols])

    @pl.when(stage == 0)
    def _():
        dw_ref[...] = jnp.zeros_like(dw_ref)
        ds_ref[...] = jnp.zeros_like(ds_ref)

    @pl.when(stage == 1)
    def _():
        last = step // 9
        i, j = 2 - step // 3, 2 - step % 3
        end = (1 - last) * (i * 3 + j) + last * 9
        final = (1 - last) * ((LO - 1 + i) * HAL + LO - 1 + j) + last * (GROUPS - 1)
        parts = [tap_rows(ga_ref, step), tap_rows(gb_ref, step), ga_ref[final], gb_ref[final], g_tails[0, end], g_tails[1, end]]
        total = jnp.dot(xt_ref[...], jnp.concatenate(parts, axis=0), preferred_element_type=F32) + dw_in[...]

        @pl.when(step < 9)
        def _():
            dw_ref[...] = total

        @pl.when(step == 9)
        def _():
            ds_ref[...] = total


def last_sums(idx, x_far, x_diag, x_tails, dzm_far, dzm_diag, vec, g_tails, sums):
    def whole(shape):
        return pl.BlockSpec(shape, lambda s, m: (0,) * len(shape))

    return pl.pallas_call(
        last_kernel,
        grid_spec=pltpu.PrefetchScalarGridSpec(
            num_scalar_prefetch=1,
            grid=(10,),
            in_specs=[
                whole((2, PIX, CHUNK)),
                whole((2, PIX, CHUNK)),
                whole((2, 2, GRP, CHUNK)),
                whole((PIX, CH)),
                whole((PIX, CH)),
                whole((3, CH)),
                whole((2, 10, GRP, CH)),
                pl.BlockSpec((None, HALF, CH), lambda s, m: (s, 0, 0)),
            ],
            out_specs=[
                pl.BlockSpec((None, None, None, HALF, CH), lambda s, m: (0, jnp.minimum(s, 8) // 3, jnp.minimum(s, 8) % 3, 0, 0)),
                pl.BlockSpec((None, HALF, CH), lambda s, m: (0, 0, 0)),
            ],
            scratch_shapes=[
                pltpu.VMEM((GROUPS, GRP, CH), BF16),
                pltpu.VMEM((GROUPS, GRP, CH), BF16),
                pltpu.VMEM((HALF, 2 * PIX + 2 * GRP), BF16),
            ],
        ),
        out_shape=[jax.ShapeDtypeStruct((1, 3, 3, HALF, CH), F32), jax.ShapeDtypeStruct((1, HALF, CH), F32)],
        compiler_params=params(1),
        cost_estimate=cost(2 * FWD_FLOPS, 2 * W_BYTES),
        name="last_sums",
    )(idx, x_far, x_diag, x_tails, dzm_far, dzm_diag, vec, g_tails, sums)


def solution(mesh):
    act_spec = P("stage", ("dp", "tp"), None, None, None)
    kernel_spec = P("stage", None, None, "tp", None)
    short_spec = P("stage", "tp", None)
    vec_spec = P("stage", "tp")
    grad_spec = P("stage", "dp", None, None, "tp")

    def device_step(act_in, w_conv, w_short, gamma, beta, gamma_s, grad_z):
        idx = jnp.stack([lax.axis_index("tp"), lax.axis_index("stage")]).astype(jnp.int32)
        w_own = w_conv.reshape(9, HALF, CH)
        s_own = w_short.reshape(HALF, CH)
        x_far, x_diag, x_tails, _, _, vec, z, z_near, dzm_far, dzm_diag, g_tails, dx, sums = main(act_in, grad_z, gamma, beta, gamma_s, w_own, s_own)
        z_out, grad_act = from_blocks(idx, z, z_near, dx)
        dw, ds = last_sums(idx, x_far, x_diag, x_tails, dzm_far, dzm_diag, vec, g_tails, sums)
        return z_out, grad_act, dw, ds

    return jax.shard_map(device_step, mesh=mesh, in_specs=(act_spec, kernel_spec, short_spec, vec_spec, vec_spec, vec_spec, grad_spec), out_specs=(grad_spec, act_spec, kernel_spec, short_spec), check_vma=False)
```

time: 222 us -> 126 us (0.57)
  waiting for transfers between devices: 53.8 us -> 0 us
  Pallas kernels: 141 us -> 124 us
  starting transfers between devices: 14.9 us -> 0 us
  local copies, waits for them, and re-layouts: 9.66 us -> 0 us
    ppermute x8 -> x0, waiting for transfers between devices: 53.8 us -> none  [the longest x1 34.6 us: block(): dzm_far = lax.ppermute(dzm, 'dp', swap)]
    pallas_call x6 -> x2, Pallas kernels: 137 us -> 120 us  [the longest x1 87.7 us: main(): pl.pallas_call(main_kernel, in_specs=[anywhere] * 2 + [vmem] * 3 + [anywh...]
    ppermute x8 -> x0, starting transfers between devices: 14.9 us -> none  [the longest x1 6.65 us: block(): dx_own = lax.ppermute(dx_half(g, w_own, s_own), 'stage', [(1, 0)])]
    unnamed x8 -> x0, local copies, waits for them, and re-layouts: 9.66 us -> none
  transfers between devices with their start and end apart: 8 -> 0, of which waited for: 3 -> 0; matrix products, arithmetic and copies ran while one was open for 2% -> 0% of each run, Pallas kernels for 28% -> 0%
where the time goes in v3:
time: 126 us; the launch traced here: 125 us
  Pallas kernels  124 us (98%)
    pallas_call x1, Pallas kernels, main(): pl.pallas_call(main_kernel, in_specs=[anywhere] * 2 + [vmem] * 3 + [anywh...  87.7 us
    pallas_call x1, Pallas kernels, last_sums(): pl.pallas_call(last_kernel, grid_spec=pltpu.PrefetchScalarGridSpec(num_sc...  32 us
    pallas_call x1, Pallas kernels, from_blocks(): pl.pallas_call(from_blocks_kernel, grid_spec=pltpu.PrefetchScalarGridSpec...  4.28 us

profile of v3, /device:TPU:2, one launch (start us, length us, event | category | flops | bytes accessed | tf_op | source)
XLA Modules:
  0.0 125.2 jit_solution(9077039127106286421)
XLA Ops:
  0.6 87.7 %main.1 = (bf16[4,784,256]{2,1,0:T(8,128)(2,1)}, bf16[2,784,256]{2,1,0:T(8,128)(2,1)}, bf16[2,2,16,256]{3,2,1,0:T(8,128)(2,1)}, bf16[9,512,1024]{2,1,0:T(8,128)(...) custom-call(bf16[1,1,28,28,1024]{4,3,2,1,0:T(8,128)(2,1)} %act.1, ...), custom_call_target="tpu_custom_call" | custom-call | flops 49325015040 | bytes 20971520 | tf_op jit(solution)/shard_map/main/pallas_call | solution.py:413
  88.3 0.6 pad_add_fusion.idx_ref
  88.9 32.0 %last_sums.1 = (f32[1,3,3,512,1024]{4,3,2,1,0:T(8,128)}, f32[1,512,1024]{2,1,0:T(8,128)}) custom-call(s32[2]{0:T(128)} %pad_add_fusion.idx_ref, bf16[4,784,256]{2,1,0:T(8,128)(2,1)} %get-tuple-element.24.xa_ref, bf16[2,784,256]{2,1,0:T(8,128)(2,1)} %get-tuple-element.25.xb_ref, bf16[2,2,16,256]{3,2,1,0:T(8,128)(2,1)} %get-tuple-element.26.x_tails, ...), custom_call_target="tpu_custom_call" | custom-call | flops 16441671680 | bytes 20971520 | tf_op jit(solution)/shard_map/last_sums/pallas_call | solution.py:506
  120.9 4.3 %from_blocks.1 = (bf16[28,28,2,512]{3,2,1,0:T(2,128)(2,1)}, bf16[1,1,28,28,1024]{4,3,2,1,0:T(8,128)(2,1)}) custom-call(s32[2]{0:T(128)} %pad_add_fusion.idx_ref, bf16[784,512]{1,0:T(8,128)(2,1)} %get-tuple-element.19.z_ref, bf16[784,512]{1,0:T(8,128)(2,1)} %get-tuple-element.20.z_near_ref, bf16[4,784,256]{2,1,0:T(8,128)(2,1)} %get-tuple-element.21.dx_ref), custom_call_target="tpu_custom_call" | custom-call | flops 411041792 | bytes 6422528 | tf_op jit(solution)/shard_map/from_blocks/pallas_call | solution.py:78

commit v4 on v3

--- a/solution.py
+++ b/solution.py
@@ -49,58 +49,6 @@
     return (col == h_hi * 56 + (w_hi * 7 + w_lo) * 2 + image).astype(F32).astype(BF16)
 
 
-def from_blocks_kernel(idx_ref, z_ref, z_near_ref, dx_ref, z_out, dx_out):
-    stage = idx_ref[1]
-
-    @pl.when(stage == 0)
-    def _():
-        z_out[...] = jnp.zeros_like(z_out)
-        select = order_matrix(True)
-        for lo in range(LO):
-            for q in range(2):
-                rows = jnp.dot(select, dx_ref[q, lo * 112:(lo + 1) * 112, :], preferred_element_type=F32).astype(BF16)
-                for hi in range(4):
-                    dx_out[hi * LO + lo, :, q * CHUNK:(q + 1) * CHUNK] = rows[hi * 32:hi * 32 + SIDE, :]
-
-    @pl.when(stage == 1)
-    def _():
-        dx_out[...] = jnp.zeros_like(dx_out)
-        select = pair_matrix(idx_ref[0], True)
-        for lo in range(LO):
-            part = slice(lo * 112, (lo + 1) * 112)
-            both = jnp.concatenate([z_ref[part, :], z_near_ref[part, :]], axis=0)
-            rows = jnp.dot(select, both, preferred_element_type=F32)
-            for hi in range(4):
-                z_out[hi * LO + lo] = rows[hi * 56:(hi + 1) * 56].astype(BF16).reshape(SIDE, 2, CHUNK)
-
-
-def from_blocks(idx, z, z_near, dx):
-    z_out, dx_out = pl.pallas_call(
-        from_blocks_kernel,
-        grid_spec=pltpu.PrefetchScalarGridSpec(
-            num_scalar_prefetch=1,
-            grid=(2,),
-            in_specs=[
-                pl.BlockSpec((PIX, CHUNK), lambda k, m: (0, k)),
-                pl.BlockSpec((PIX, CHUNK), lambda k, m: (0, k)),
-                pl.BlockSpec((2, PIX, CHUNK), lambda k, m: (k, 0, 0)),
-            ],
-            out_specs=[
-                pl.BlockSpec((SIDE, SIDE, 2, CHUNK), lambda k, m: (0, 0, 0, k)),
-                pl.BlockSpec((None, None, SIDE, SIDE, HALF), lambda k, m: (0, 0, 0, 0, (m[0] + k) % 2)),
-            ],
-        ),
-        out_shape=[
-            jax.ShapeDtypeStruct((SIDE, SIDE, 2, HALF), BF16),
-            jax.ShapeDtypeStruct((1, 1, SIDE, SIDE, CH), BF16),
-        ],
-        compiler_params=params(1),
-        cost_estimate=cost(2 * 2 * 7 * 112 * 128 * HALF * 2, 4 * 2 * PIX * HALF * 2),
-        name="from_blocks",
-    )(idx, z, z_near, dx)
-    return jnp.transpose(z_out, (2, 0, 1, 3))[None], dx_out
-
-
 def moved(tile, step_h, step_w):
     wide = tile.astype(F32)
     n = wide.shape[1]
@@ -138,11 +86,6 @@
     return whole.reshape(PIX, whole.shape[-1])
 
 
-def both_grads(dz, vec_ref, g_ref):
-    g_ref[HAL * HAL:] = (dz * vec_ref[2:3, :]).astype(BF16).reshape(LO * LO, GRP, -1)
-    fill_halo(g_ref, (dz * vec_ref[0:1, :]).astype(BF16))
-
-
 FWD_FLOPS = 2 * PIX * HALF * CH * 10
 W_BYTES = 10 * HALF * CH * 2
 
@@ -163,7 +106,7 @@
     act, grad, gam, bet, gms, w_own, s_own,
     x_far, x_diag, x_tails, w_peer, s_peer, vec_out, z_out, z_near, dzm_far, dzm_diag, g_tails, dx_in, sums,
     act_in, pad, xs, xr, xn, xh, im, w_buf, s_buf, pre, short, grad_in, dz_own, dz_send, dz_peer, vec_peer, z_st, dzm_st, g_st, g_near,
-    act_sem, x_sem, far_sem, hop_sem, near_sem, diag_sem, w_sem, vec_sem, peer_sem, dzm_sem, dx_sem, w_local, keep_sem, tail_sem, out_sem, sum_sem,
+    act_sem, x_sem, far_sem, hop_sem, near_sem, diag_sem, w_sem, vec_sem, peer_sem, g_sem, dzm_sem, dx_sem, w_local, keep_sem, tail_sem, out_sem, sum_sem,
 ):
     t = lax.axis_index("tp")
     stage = lax.axis_index("stage")
@@ -259,18 +202,20 @@
         def near_copy(q):
             return remote(xr.at[q], xn.at[q - 2], near_sem.at[q - 2], peer)
 
-        def chunk(q, carry):
+        def land(q):
             x_copy(q).wait_recv()
-
-            @pl.when(q >= 2)
-            def _():
-                near_copy(q).start()
-
             fill_halo(xh, xr[q])
             for i in range(3):
                 for j in range(3):
                     k = i * 3 + j
                     im[:, k * CHUNK:(k + 1) * CHUNK] = window(xh, i, j)
+
+        def terms(q, cols):
+            main = jnp.dot(im[...], w_buf[q, :, :, cols].reshape(9 * CHUNK, HALF), preferred_element_type=F32)
+            return main, jnp.dot(xr[q], s_buf[q, :, cols], preferred_element_type=F32)
+
+        def chunk(q, carry):
+            land(q)
 
             @pl.when(q == 1)
             def _():
@@ -280,12 +225,15 @@
                     for copy in w_fetch(w_peer, s_peer, k, k + 2):
                         copy.start()
 
+            @pl.when(q == 2)
+            def _():
+                near_copy(q).start()
+
             for copy in w_fetch(w_own, s_own, 0, q):
                 copy.wait()
             for n in range(2):
                 cols = slice(n * HALF, (n + 1) * HALF)
-                main = jnp.dot(im[...], w_buf[q, :, :, cols].reshape(9 * CHUNK, HALF), preferred_element_type=F32)
-                side = jnp.dot(xr[q], s_buf[q, :, cols], preferred_element_type=F32)
+                main, side = terms(q, cols)
 
                 @pl.when(q == 0)
                 def _():
@@ -299,33 +247,48 @@
 
             return carry
 
-        lax.fori_loop(0, N_CHUNKS, chunk, 0)
+        lax.fori_loop(0, N_CHUNKS - 1, chunk, 0)
 
         for copy in vec_copies:
             copy.wait_recv()
         dz_copy.wait_recv()
-        for n in range(CH // TILE):
-            half, part = n // 2, slice((n % 2) * TILE, (n % 2 + 1) * TILE)
-            cols = slice(n * TILE, (n + 1) * TILE)
+
+        def dzm_copy(n):
+            cols = slice(n * HALF, (n + 1) * HALF)
+            return remote(dzm_st.at[:, cols], dzm_far.at[:, cols], dzm_sem.at[n], other_dp)
+
+        def g_copy(n):
+            cols = slice(n * HALF, (n + 1) * HALF)
+            return remote(g_st.at[:, :, cols], g_near.at[:, :, cols], g_sem.at[n], peer)
+
+        land(N_CHUNKS - 1)
+        near_copy(3).start()
+        for copy in w_fetch(w_own, s_own, 0, 3):
+            copy.wait()
+        for half in range(2):
             mine = t == half
-            gamma, beta, gamma_s = (jnp.where(mine, ref[:, part], vec_peer[k, :, part]) for k, ref in enumerate((gam, bet, gms)))
-            for k, row in enumerate((gamma, beta, gamma_s)):
-                vec_out[k:k + 1, cols] = row
-            u = pre[:, cols] * gamma + beta + short[:, cols] * gamma_s
-            z_st[:, cols] = jnp.maximum(u, 0.0).astype(BF16)
-            dz = jnp.where(mine, dz_own[:, part].astype(F32), dz_peer[:, part].astype(F32))
-            dz = jnp.where(u > 0.0, dz, 0.0)
-            dzm_st[:, cols] = dz.astype(BF16)
-            g_st[HAL * HAL:, :, cols] = (dz * gamma_s).astype(BF16).reshape(LO * LO, GRP, TILE)
-            fill_halo(g_st.at[:, :, cols], (dz * gamma).astype(BF16))
-
-        dzm_copy = remote(dzm_st, dzm_far, dzm_sem.at[0], other_dp)
-        g_copy = remote(g_st, g_near, peer_sem.at[1], peer)
+            main, side = terms(N_CHUNKS - 1, slice(half * HALF, (half + 1) * HALF))
+            for n in range(2):
+                part = slice(n * TILE, (n + 1) * TILE)
+                cols = slice(half * HALF + n * TILE, half * HALF + (n + 1) * TILE)
+                gamma, beta, gamma_s = (jnp.where(mine, ref[:, part], vec_peer[k, :, part]) for k, ref in enumerate((gam, bet, gms)))
+                for k, row in enumerate((gamma, beta, gamma_s)):
+                    vec_out[k:k + 1, cols] = row
+                u = (pre[:, cols] + main[:, part]) * gamma + beta + (short[:, cols] + side[:, part]) * gamma_s
+                z_st[:, cols] = jnp.maximum(u, 0.0).astype(BF16)
+                dz = jnp.where(mine, dz_own[:, part].astype(F32), dz_peer[:, part].astype(F32))
+                dz = jnp.where(u > 0.0, dz, 0.0)
+                dzm_st[:, cols] = dz.astype(BF16)
+                g_st[HAL * HAL:, :, cols] = (dz * gamma_s).astype(BF16).reshape(LO * LO, GRP, TILE)
+                fill_halo(g_st.at[:, :, cols], (dz * gamma).astype(BF16))
+            dzm_copy(half).start()
+            g_copy(half).start()
+
         mine_at, theirs_at = pl.multiple_of(t * HALF, HALF), pl.multiple_of((1 - t) * HALF, HALF)
         z_copy = remote(z_st.at[:, pl.ds(theirs_at, HALF)], z_near, peer_sem.at[2], peer)
         z_keep = pltpu.make_async_copy(z_st.at[:, pl.ds(mine_at, HALF)], z_out, keep_sem)
-        for copy in (dzm_copy, g_copy, z_copy, z_keep):
-            copy.start()
+        z_copy.start()
+        z_keep.start()
 
         def dx_chunk(q, carry):
             total = dot_nt(g_st[HAL * HAL:].reshape(PIX, CH), s_buf[q])
@@ -339,7 +302,8 @@
 
         near_copy(2).wait_recv()
         near_copy(3).wait_recv()
-        g_copy.wait_recv()
+        g_copy(0).wait_recv()
+        g_copy(1).wait_recv()
         tails = []
         for k, (x_ref, g_ref) in enumerate(((xr, g_st), (xn, g_near))):
             tails.append(pltpu.make_async_copy(x_ref.at[0:2, MAIN:PIX], x_tails.at[k], tail_sem.at[k, 0]))
@@ -357,7 +321,7 @@
         def diag_copy(k):
             return remote(x_far.at[2 + k], x_diag.at[k], diag_sem.at[k], peer)
 
-        dzm_diag_copy = remote(dzm_far, dzm_diag, dzm_sem.at[1], peer)
+        dzm_diag_copy = remote(dzm_far, dzm_diag, dzm_sem.at[2], peer)
 
         def sum_copy(tap, k):
             return pltpu.make_async_copy((pre, short)[k].at[:HALF], sums.at[tap], sum_sem.at[k])
@@ -371,7 +335,8 @@
 
             @pl.when(p == 4)
             def _():
-                dzm_copy.wait_recv()
+                dzm_copy(0).wait_recv()
+                dzm_copy(1).wait_recv()
                 dzm_diag_copy.start()
 
             for k in range(2):
@@ -401,7 +366,7 @@
         z_keep.wait()
         z_copy.wait()
         dzm_diag_copy.wait()
-        for copy in [w_copy, s_copy, dz_copy, dzm_copy, g_copy] + vec_copies:
+        for copy in [w_copy, s_copy, dz_copy, dzm_copy(0), dzm_copy(1), g_copy(0), g_copy(1)] + vec_copies:
             copy.wait_send()
 
 
@@ -450,7 +415,7 @@
             pltpu.VMEM((PIX, CH), BF16),
             pltpu.VMEM((GROUPS, GRP, CH), BF16),
             pltpu.VMEM((GROUPS, GRP, CH), BF16),
-            dma((5,)), dma((4, 2)), dma((4, 2)), dma((4, 2)), dma((2, 2)), dma((2, 2)), dma((2, 2)), dma((3, 2)), dma((3, 2)), dma((2, 2)),
+            dma((5,)), dma((4, 2)), dma((4, 2)), dma((4, 2)), dma((2, 2)), dma((2, 2)), dma((2, 2)), dma((3, 2)), dma((3, 2)), dma((2, 2)), dma((3, 2)),
             dma((4, 2)), dma((4, 2)), dma, dma((2, 5)), dma, dma((2,)),
         ],
         compiler_params=pltpu.CompilerParams(collective_id=0, has_side_effects=True, vmem_limit_bytes=66 * 1000 * 1000),
@@ -459,80 +424,200 @@
     )(act_in, jnp.transpose(grad_z[0], (1, 2, 0, 3)), gamma, beta, gamma_s, w_own, s_own)
 
 
-def last_kernel(idx_ref, xa_ref, xb_ref, x_tails, dza_ref, dzb_ref, vec_ref, g_tails, dw_in, dw_ref, ds_ref, ga_ref, gb_ref, xt_ref):
+SLOTS = 4
+
+
+def last_kernel(
+    xa, xb, x_tails, dza, dzb, vec_ref, g_tails, sums, z, z_near, dx,
+    dw_out, ds_out, z_out, dx_out,
+    xa_v, xb_v, dza_v, dzb_v, sum_v, tot_v, z_v, zn_v, dx_v, z_st, dx_st, ga_ref, gb_ref, gsa_ref, gsb_ref, xt_ref, in_sem, sum_sem, tot_sem, side_sem, out_sem,
+):
     step = pl.program_id(0)
-    stage = idx_ref[1]
+    t = lax.axis_index("tp")
+    stage = lax.axis_index("stage")
+    fetches = [
+        pltpu.make_async_copy(src, dst, in_sem.at[k])
+        for k, (src, dst) in enumerate(((xa.at[0:2], xa_v), (dza, dza_v), (xb, xb_v), (dzb, dzb_v)))
+    ]
+    sides = [pltpu.make_async_copy(src, dst, side_sem.at[k]) for k, (src, dst) in enumerate(((z, z_v), (z_near, zn_v), (dx, dx_v)))]
+    outs = [pltpu.make_async_copy(src, dst, out_sem.at[k]) for k, (src, dst) in enumerate(((z_st, z_out), (dx_st, dx_out)))]
+
+    def sum_fetch(term):
+        return pltpu.make_async_copy(sums.at[(term + 9) % 10], sum_v.at[term % SLOTS], sum_sem.at[term % SLOTS])
+
+    def tot_copy(term):
+        tap = term - 1
+        return pltpu.make_async_copy(tot_v.at[term % SLOTS], dw_out.at[0, tap // 3, tap % 3], tot_sem.at[term % SLOTS])
+
+    short_copy = pltpu.make_async_copy(tot_v.at[0], ds_out.at[0], tot_sem.at[0])
+
+    def product(parts):
+        return jnp.dot(xt_ref[...], jnp.concatenate(parts, axis=0), preferred_element_type=F32)
+
+    def tap_product(tap):
+        i, j = 2 - tap // 3, 2 - tap % 3
+        final = (LO - 1 + i) * HAL + LO - 1 + j
+        end = i * 3 + j
+        return product([tap_rows(ga_ref, tap), tap_rows(gb_ref, tap), ga_ref[final], gb_ref[final], g_tails[0, end], g_tails[1, end]])
 
     @pl.when((step == 0) & (stage == 1))
     def _():
+        for copy in fetches:
+            copy.start()
+        images = ((xa_v, dza_v, ga_ref, gsa_ref), (xb_v, dzb_v, gb_ref, gsb_ref))
+        for k, (x_v, dz_v, g_ref, gs_ref) in enumerate(images):
+            fetches[2 * k].wait()
+            for q in range(2):
+                rows = slice(q * CHUNK, (q + 1) * CHUNK)
+                xt_ref[rows, k * MAIN:(k + 1) * MAIN] = x_v[q, :MAIN, :].T
+            fetches[2 * k + 1].wait()
+            if k == 0:
+                sum_fetch(0).start()
+                sum_fetch(1).start()
+            gs_ref[...] = (dz_v[...].astype(F32) * vec_ref[2:3, :]).astype(BF16)
+        sides[0].start()
+        sides[1].start()
+        sum_fetch(2).start()
+        sum_fetch(3).start()
         for q in range(2):
             rows = slice(q * CHUNK, (q + 1) * CHUNK)
-            xt_ref[rows, :MAIN] = xa_ref[q, :MAIN, :].T
-            xt_ref[rows, MAIN:2 * MAIN] = xb_ref[q, :MAIN, :].T
-            ends = [xa_ref[q, MAIN:, :], xb_ref[q, MAIN:, :], x_tails[0, q], x_tails[1, q]]
+            ends = [xa_v[q, MAIN:, :], xb_v[q, MAIN:, :], x_tails[0, q], x_tails[1, q]]
             xt_ref[rows, 2 * MAIN:] = jnp.concatenate(ends, axis=0).T
-        for dz_ref, g_ref in ((dza_ref, ga_ref), (dzb_ref, gb_ref)):
+        sum_fetch(0).wait()
+        sum_fetch(1).wait()
+        total = product([gsa_ref[:MAIN], gsb_ref[:MAIN], gsa_ref[MAIN:], gsb_ref[MAIN:], g_tails[0, 9], g_tails[1, 9]])
+        for x_v, dz_v, g_ref, gs_ref in images:
             for n in range(CH // TILE):
                 cols = slice(n * TILE, (n + 1) * TILE)
-                both_grads(dz_ref[:, cols].astype(F32), vec_ref.at[:, cols], g_ref.at[:, :, cols])
-
-    @pl.when(stage == 0)
-    def _():
-        dw_ref[...] = jnp.zeros_like(dw_ref)
-        ds_ref[...] = jnp.zeros_like(ds_ref)
-
-    @pl.when(stage == 1)
-    def _():
-        last = step // 9
-        i, j = 2 - step // 3, 2 - step % 3
-        end = (1 - last) * (i * 3 + j) + last * 9
-        final = (1 - last) * ((LO - 1 + i) * HAL + LO - 1 + j) + last * (GROUPS - 1)
-        parts = [tap_rows(ga_ref, step), tap_rows(gb_ref, step), ga_ref[final], gb_ref[final], g_tails[0, end], g_tails[1, end]]
-        total = jnp.dot(xt_ref[...], jnp.concatenate(parts, axis=0), preferred_element_type=F32) + dw_in[...]
-
-        @pl.when(step < 9)
+                fill_halo(g_ref.at[:, :, cols], (dz_v[:, cols].astype(F32) * vec_ref[0:1, cols]).astype(BF16))
+        tot_v[0] = total + sum_v[0]
+        short_copy.start()
+        tot_v[1] = tap_product(0) + sum_v[1]
+        tot_copy(1).start()
+
+    def drain(term):
+        @pl.when(term == 4)
         def _():
-            dw_ref[...] = total
-
-        @pl.when(step == 9)
+            short_copy.wait()
+
+        @pl.when(term != 4)
         def _():
-            ds_ref[...] = total
-
-
-def last_sums(idx, x_far, x_diag, x_tails, dzm_far, dzm_diag, vec, g_tails, sums):
+            tot_copy(term - SLOTS).wait()
+
+    @pl.when((step > 0) & (stage == 1))
+    def _():
+        @pl.when(step < 4)
+        def _():
+            sum_fetch(2 * step + 2).start()
+            sum_fetch(2 * step + 3).start()
+
+        @pl.when(step > 1)
+        def _():
+            drain(2 * step)
+            drain(2 * step + 1)
+
+        sum_fetch(2 * step).wait()
+        sum_fetch(2 * step + 1).wait()
+        for k in range(2):
+            term = 2 * step + k
+            tot_v[term % SLOTS] = tap_product(term - 1) + sum_v[term % SLOTS]
+        tot_copy(2 * step).start()
+        tot_copy(2 * step + 1).start()
+
+    @pl.when((step == 0) & (stage == 0))
+    def _():
+        sides[2].start()
+        z_st[...] = jnp.zeros_like(z_st)
+        outs[0].start()
+        tot_v[0] = jnp.zeros_like(tot_v[0])
+        short_copy.start()
+        short_copy.wait()
+        sides[2].wait()
+        select = order_matrix(True)
+        for lo in range(LO):
+            for q in range(N_CHUNKS):
+                to = pl.multiple_of(lax.rem(t * HALF + q * CHUNK, CH), CHUNK)
+                rows = jnp.dot(select, dx_v[q, lo * 112:(lo + 1) * 112, :], preferred_element_type=F32).astype(BF16)
+                for hi in range(4):
+                    dx_st[0, 0, hi * LO + lo, :, pl.ds(to, CHUNK)] = rows[hi * 32:hi * 32 + SIDE, :]
+        outs[1].start()
+
+        def clear(tap, carry):
+            copy = pltpu.make_async_copy(tot_v.at[0], dw_out.at[0, tap // 3, tap % 3], tot_sem.at[0])
+            copy.start()
+            copy.wait()
+            return carry
+
+        lax.fori_loop(0, 9, clear, 0)
+
+    @pl.when((step == 1) & (stage == 1))
+    def _():
+        dx_st[...] = jnp.zeros_like(dx_st)
+        outs[1].start()
+        for copy in sides[:2]:
+            copy.wait()
+        select = pair_matrix(t, True)
+        for lo in range(LO):
+            part = slice(lo * 112, (lo + 1) * 112)
+            both = jnp.concatenate([z_v[part, :], zn_v[part, :]], axis=0)
+            rows = jnp.dot(select, both, preferred_element_type=F32)
+            for hi in range(4):
+                z_st[hi * LO + lo] = rows[hi * 56:(hi + 1) * 56].astype(BF16).reshape(SIDE, 2, HALF)
+        outs[0].start()
+
+    @pl.when(step == 4)
+    def _():
+        for copy in outs:
+            copy.wait()
+
+    @pl.when((step == 4) & (stage == 1))
+    def _():
+        for term in range(6, 10):
+            tot_copy(term).wait()
+
+
+def last(x_far, x_diag, x_tails, dzm_far, dzm_diag, vec, g_tails, sums, z, z_near, dx):
     def whole(shape):
-        return pl.BlockSpec(shape, lambda s, m: (0,) * len(shape))
-
-    return pl.pallas_call(
+        return pl.BlockSpec(shape, lambda s: (0,) * len(shape))
+
+    anywhere = pl.BlockSpec(memory_space=pl.ANY)
+    dma = pltpu.SemaphoreType.DMA
+    z_shape, dx_shape = (SIDE, SIDE, 2, HALF), (1, 1, SIDE, SIDE, CH)
+    dw, ds, z_out, dx_out = pl.pallas_call(
         last_kernel,
-        grid_spec=pltpu.PrefetchScalarGridSpec(
-            num_scalar_prefetch=1,
-            grid=(10,),
-            in_specs=[
-                whole((2, PIX, CHUNK)),
-                whole((2, PIX, CHUNK)),
-                whole((2, 2, GRP, CHUNK)),
-                whole((PIX, CH)),
-                whole((PIX, CH)),
-                whole((3, CH)),
-                whole((2, 10, GRP, CH)),
-                pl.BlockSpec((None, HALF, CH), lambda s, m: (s, 0, 0)),
-            ],
-            out_specs=[
-                pl.BlockSpec((None, None, None, HALF, CH), lambda s, m: (0, jnp.minimum(s, 8) // 3, jnp.minimum(s, 8) % 3, 0, 0)),
-                pl.BlockSpec((None, HALF, CH), lambda s, m: (0, 0, 0)),
-            ],
-            scratch_shapes=[
-                pltpu.VMEM((GROUPS, GRP, CH), BF16),
-                pltpu.VMEM((GROUPS, GRP, CH), BF16),
-                pltpu.VMEM((HALF, 2 * PIX + 2 * GRP), BF16),
-            ],
-        ),
-        out_shape=[jax.ShapeDtypeStruct((1, 3, 3, HALF, CH), F32), jax.ShapeDtypeStruct((1, HALF, CH), F32)],
+        grid=(5,),
+        in_specs=[anywhere, anywhere, whole((2, 2, GRP, CHUNK)), anywhere, anywhere, whole((3, CH)), whole((2, 10, GRP, CH))] + [anywhere] * 4,
+        out_specs=[anywhere] * 4,
+        out_shape=[
+            jax.ShapeDtypeStruct((1, 3, 3, HALF, CH), F32),
+            jax.ShapeDtypeStruct((1, HALF, CH), F32),
+            jax.ShapeDtypeStruct(z_shape, BF16),
+            jax.ShapeDtypeStruct(dx_shape, BF16),
+        ],
+        scratch_shapes=[
+            pltpu.VMEM((2, PIX, CHUNK), BF16),
+            pltpu.VMEM((2, PIX, CHUNK), BF16),
+            pltpu.VMEM((PIX, CH), BF16),
+            pltpu.VMEM((PIX, CH), BF16),
+            pltpu.VMEM((SLOTS, HALF, CH), F32),
+            pltpu.VMEM((SLOTS, HALF, CH), F32),
+            pltpu.VMEM((PIX, HALF), BF16),
+            pltpu.VMEM((PIX, HALF), BF16),
+            pltpu.VMEM((N_CHUNKS, PIX, CHUNK), BF16),
+            pltpu.VMEM(z_shape, BF16),
+            pltpu.VMEM(dx_shape, BF16),
+            pltpu.VMEM((HAL * HAL, GRP, CH), BF16),
+            pltpu.VMEM((HAL * HAL, GRP, CH), BF16),
+            pltpu.VMEM((PIX, CH), BF16),
+            pltpu.VMEM((PIX, CH), BF16),
+            pltpu.VMEM((HALF, 2 * PIX + 2 * GRP), BF16),
+            dma((4,)), dma((SLOTS,)), dma((SLOTS,)), dma((3,)), dma((2,)),
+        ],
         compiler_params=params(1),
         cost_estimate=cost(2 * FWD_FLOPS, 2 * W_BYTES),
-        name="last_sums",
-    )(idx, x_far, x_diag, x_tails, dzm_far, dzm_diag, vec, g_tails, sums)
+        name="last",
+    )(x_far, x_diag, x_tails, dzm_far, dzm_diag, vec, g_tails, sums, z, z_near, dx)
+    return jnp.transpose(z_out, (2, 0, 1, 3))[None], dx_out, dw, ds
 
 
 def solution(mesh):
@@ -543,12 +628,9 @@
     grad_spec = P("stage", "dp", None, None, "tp")
 
     def device_step(act_in, w_conv, w_short, gamma, beta, gamma_s, grad_z):
-        idx = jnp.stack([lax.axis_index("tp"), lax.axis_index("stage")]).astype(jnp.int32)
         w_own = w_conv.reshape(9, HALF, CH)
         s_own = w_short.reshape(HALF, CH)
         x_far, x_diag, x_tails, _, _, vec, z, z_near, dzm_far, dzm_diag, g_tails, dx, sums = main(act_in, grad_z, gamma, beta, gamma_s, w_own, s_own)
-        z_out, grad_act = from_blocks(idx, z, z_near, dx)
-        dw, ds = last_sums(idx, x_far, x_diag, x_tails, dzm_far, dzm_diag, vec, g_tails, sums)
-        return z_out, grad_act, dw, ds
+        return last(x_far, x_diag, x_tails, dzm_far, dzm_diag, vec, g_tails, sums, z, z_near, dx)
 
     return jax.shard_map(device_step, mesh=mesh, in_specs=(act_spec, kernel_spec, short_spec, vec_spec, vec_spec, vec_spec, grad_spec), out_specs=(grad_spec, act_spec, kernel_spec, short_spec), check_vma=False)

time: 126 us -> 117 us (0.929)
  Pallas kernels: 124 us -> 116 us
    pallas_call x2 -> x1, Pallas kernels: 36.3 us -> 28.3 us  [last(): pl.pallas_call(last_kernel, grid=(5,), in_specs=[anywhere, anywhere, whol...]
where the time goes in v4:
time: 117 us; the launch traced here: 116 us
  Pallas kernels  116 us (99%)
    pallas_call x1, Pallas kernels, main(): pl.pallas_call(main_kernel, in_specs=[anywhere] * 2 + [vmem] * 3 + [anywh...  87.2 us
    pallas_call x1, Pallas kernels, last(): pl.pallas_call(last_kernel, grid=(5,), in_specs=[anywhere, anywhere, whol...  28.3 us

profile of v4, /device:TPU:2, one launch (start us, length us, event | category | flops | bytes accessed | tf_op | source)
XLA Modules:
  0.0 116.3 jit_solution(9813602446749943706)
XLA Ops:
  0.6 87.2 %main.1 = (bf16[4,784,256]{2,1,0:T(8,128)(2,1)}, bf16[2,784,256]{2,1,0:T(8,128)(2,1)}, bf16[2,2,16,256]{3,2,1,0:T(8,128)(2,1)}, bf16[9,512,1024]{2,1,0:T(8,128)(...) custom-call(bf16[1,1,28,28,1024]{4,3,2,1,0:T(8,128)(2,1)} %act.1, ...), custom_call_target="tpu_custom_call" | custom-call | flops 49325015040 | bytes 20971520 | tf_op jit(solution)/shard_map/main/pallas_call | solution.py:378
  87.8 28.3 %last.1 = (f32[1,3,3,512,1024]{4,3,2,1,0:T(8,128)}, f32[1,512,1024]{2,1,0:T(8,128)}, bf16[28,28,2,512]{3,2,1,0:T(2,128)(2,1)}, bf16[1,1,28,28,1024]{4,3,2,1,0:T(8,128)(2,1)}) custom-call(bf16[4,784,256]{2,1,0:T(8,128)(2,1)} %get-tuple-element.19.xa, bf16[2,784,256]{2,1,0:T(8,128)(2,1)} %get-tuple-element.20.xb, ...), custom_call_target="tpu_custom_call" | custom-call | flops 16441671680 | bytes 20971520 | tf_op jit(solution)/shard_map/last/pallas_call | solution.py:586

commit v5 on v4

--- a/solution.py
+++ b/solution.py
@@ -15,6 +15,7 @@
 CH = 1024
 TILE = 256
 CHUNK = 256
+PART = CHUNK // 2
 N_CHUNKS = CH // CHUNK
 MAIN = 768
 MESH = pl.DeviceIdType.MESH
@@ -140,6 +141,20 @@
     barrier = pltpu.get_barrier_semaphore()
     for target in ({"tp": 1 - t}, {"stage": 1 - stage}, {"dp": 1 - dp}):
         pl.semaphore_signal(barrier, inc=1, device_id=target, device_id_type=MESH)
+
+    def arrange(q):
+        select = order_matrix(False)
+        act_copy(q).wait()
+        pad[:, :SIDE, :] = act_in[q]
+        for lo in range(LO):
+            rows = jnp.concatenate([pad[hi * LO + lo] for hi in range(4)], axis=0)
+            xs[q, lo * 112:(lo + 1) * 112, :] = jnp.dot(select, rows, preferred_element_type=F32).astype(BF16)
+
+    @pl.when(stage == 0)
+    def _():
+        pad[...] = jnp.zeros_like(pad)
+        arrange(0)
+
     pl.semaphore_wait(barrier, 3)
 
     def remote(src, dst, sems, target):
@@ -150,6 +165,10 @@
     def x_copy(q):
         return remote(xs.at[q], xr.at[q], x_sem.at[q], other_stage)
 
+    def end_copy(k):
+        cols = slice(k * PART, (k + 1) * PART)
+        return remote(xs.at[N_CHUNKS - 1, :, cols], xr.at[N_CHUNKS - 1, :, cols], x_sem.at[N_CHUNKS - 1 + k], other_stage)
+
     def far_copy(q):
         return remote(xs.at[q], xr.at[q], far_sem.at[q], other_dp)
 
@@ -161,23 +180,26 @@
 
     @pl.when(stage == 0)
     def _():
-        pad[...] = jnp.zeros_like(pad)
-        select = order_matrix(False)
         for q in range(N_CHUNKS):
-            act_copy(q).wait()
-            pad[:, :SIDE, :] = act_in[q]
-            for lo in range(LO):
-                rows = jnp.concatenate([pad[hi * LO + lo] for hi in range(4)], axis=0)
-                xs[q, lo * 112:(lo + 1) * 112, :] = jnp.dot(select, rows, preferred_element_type=F32).astype(BF16)
-            x_copy(q).start()
+            if q:
+                arrange(q)
+            if q < N_CHUNKS - 1:
+                x_copy(q).start()
+            else:
+                end_copy(0).start()
+                end_copy(1).start()
             far_copy(q).start()
         for q in range(N_CHUNKS):
             far_copy(q).wait_recv()
             hop_copy(q).start()
+        for k in range(2):
+            end_copy(k).wait_send()
         for q in range(N_CHUNKS):
-            x_copy(q).wait_send()
+            if q < N_CHUNKS - 1:
+                x_copy(q).wait_send()
             far_copy(q).wait_send()
             hop_copy(q).wait_send()
+        for q in range(N_CHUNKS):
             dx_copy(q).wait_recv()
 
     @pl.when(stage == 1)
@@ -202,20 +224,25 @@
         def near_copy(q):
             return remote(xr.at[q], xn.at[q - 2], near_sem.at[q - 2], peer)
 
-        def land(q):
-            x_copy(q).wait_recv()
-            fill_halo(xh, xr[q])
+        def land(q, cols):
+            n = cols.stop - cols.start
+            halo = xh.at[:, :, :n]
+            fill_halo(halo, xr[q, :, cols])
             for i in range(3):
                 for j in range(3):
                     k = i * 3 + j
-                    im[:, k * CHUNK:(k + 1) * CHUNK] = window(xh, i, j)
-
-        def terms(q, cols):
-            main = jnp.dot(im[...], w_buf[q, :, :, cols].reshape(9 * CHUNK, HALF), preferred_element_type=F32)
-            return main, jnp.dot(xr[q], s_buf[q, :, cols], preferred_element_type=F32)
+                    im[:, k * n:(k + 1) * n] = window(halo, i, j)
+
+        def terms(q, rows, cols):
+            k = 9 * (rows.stop - rows.start)
+            main = jnp.dot(im[:, :k], w_buf[q, :, rows, cols].reshape(k, HALF), preferred_element_type=F32)
+            return main, jnp.dot(xr[q, :, rows], s_buf[q, rows, cols], preferred_element_type=F32)
+
+        whole = slice(0, CHUNK)
 
         def chunk(q, carry):
-            land(q)
+            x_copy(q).wait_recv()
+            land(q, whole)
 
             @pl.when(q == 1)
             def _():
@@ -233,7 +260,7 @@
                 copy.wait()
             for n in range(2):
                 cols = slice(n * HALF, (n + 1) * HALF)
-                main, side = terms(q, cols)
+                main, side = terms(q, whole, cols)
 
                 @pl.when(q == 0)
                 def _():
@@ -261,13 +288,21 @@
             cols = slice(n * HALF, (n + 1) * HALF)
             return remote(g_st.at[:, :, cols], g_near.at[:, :, cols], g_sem.at[n], peer)
 
-        land(N_CHUNKS - 1)
-        near_copy(3).start()
         for copy in w_fetch(w_own, s_own, 0, 3):
             copy.wait()
+        end_copy(0).wait_recv()
+        land(N_CHUNKS - 1, slice(0, PART))
+        for n in range(2):
+            cols = slice(n * HALF, (n + 1) * HALF)
+            main, side = terms(N_CHUNKS - 1, slice(0, PART), cols)
+            pre[:, cols] += main
+            short[:, cols] += side
+        end_copy(1).wait_recv()
+        land(N_CHUNKS - 1, slice(PART, CHUNK))
+        near_copy(3).start()
         for half in range(2):
             mine = t == half
-            main, side = terms(N_CHUNKS - 1, slice(half * HALF, (half + 1) * HALF))
+            main, side = terms(N_CHUNKS - 1, slice(PART, CHUNK), slice(half * HALF, (half + 1) * HALF))
             for n in range(2):
                 part = slice(n * TILE, (n + 1) * TILE)
                 cols = slice(half * HALF + n * TILE, half * HALF + (n + 1) * TILE)
@@ -321,23 +356,25 @@
         def diag_copy(k):
             return remote(x_far.at[2 + k], x_diag.at[k], diag_sem.at[k], peer)
 
-        dzm_diag_copy = remote(dzm_far, dzm_diag, dzm_sem.at[2], peer)
+        def dzm_diag_copy(n):
+            cols = slice(n * HALF, (n + 1) * HALF)
+            return remote(dzm_far.at[:, cols], dzm_diag.at[:, cols], dzm_sem.at[2 + n], peer)
 
         def sum_copy(tap, k):
             return pltpu.make_async_copy((pre, short)[k].at[:HALF], sums.at[tap], sum_sem.at[k])
 
         def sum_pair(p, carry):
-            @pl.when(p == 2)
+            @pl.when(p == 4)
             def _():
                 for k in range(2):
                     hop_copy(2 + k).wait_recv()
                     diag_copy(k).start()
 
-            @pl.when(p == 4)
-            def _():
-                dzm_copy(0).wait_recv()
-                dzm_copy(1).wait_recv()
-                dzm_diag_copy.start()
+            for n in range(2):
+                @pl.when(p == 3 + n)
+                def _():
+                    dzm_copy(n).wait_recv()
+                    dzm_diag_copy(n).start()
 
             for k in range(2):
                 tap = 2 * p + k
@@ -365,7 +402,8 @@
             copy.wait()
         z_keep.wait()
         z_copy.wait()
-        dzm_diag_copy.wait()
+        for n in range(2):
+            dzm_diag_copy(n).wait()
         for copy in [w_copy, s_copy, dz_copy, dzm_copy(0), dzm_copy(1), g_copy(0), g_copy(1)] + vec_copies:
             copy.wait_send()
 
@@ -415,7 +453,7 @@
             pltpu.VMEM((PIX, CH), BF16),
             pltpu.VMEM((GROUPS, GRP, CH), BF16),
             pltpu.VMEM((GROUPS, GRP, CH), BF16),
-            dma((5,)), dma((4, 2)), dma((4, 2)), dma((4, 2)), dma((2, 2)), dma((2, 2)), dma((2, 2)), dma((3, 2)), dma((3, 2)), dma((2, 2)), dma((3, 2)),
+            dma((5,)), dma((5, 2)), dma((4, 2)), dma((4, 2)), dma((2, 2)), dma((2, 2)), dma((2, 2)), dma((3, 2)), dma((3, 2)), dma((2, 2)), dma((4, 2)),
             dma((4, 2)), dma((4, 2)), dma, dma((2, 5)), dma, dma((2,)),
         ],
         compiler_params=pltpu.CompilerParams(collective_id=0, has_side_effects=True, vmem_limit_bytes=66 * 1000 * 1000),
@@ -428,9 +466,9 @@
 
 
 def last_kernel(
-    xa, xb, x_tails, dza, dzb, vec_ref, g_tails, sums, z, z_near, dx,
+    xa, xb, x_ends, dza, dzb, vec, g_ends, sums, z, z_near, dx,
     dw_out, ds_out, z_out, dx_out,
-    xa_v, xb_v, dza_v, dzb_v, sum_v, tot_v, z_v, zn_v, dx_v, z_st, dx_st, ga_ref, gb_ref, gsa_ref, gsb_ref, xt_ref, in_sem, sum_sem, tot_sem, side_sem, out_sem,
+    xa_v, xb_v, dza_v, dzb_v, x_tails, vec_ref, g_tails, sum_v, tot_v, z_v, zn_v, dx_v, z_st, dx_st, ga_ref, gb_ref, gsa_ref, gsb_ref, xt_ref, in_sem, small_sem, sum_sem, tot_sem, side_sem, out_sem,
 ):
     step = pl.program_id(0)
     t = lax.axis_index("tp")
@@ -439,6 +477,7 @@
         pltpu.make_async_copy(src, dst, in_sem.at[k])
         for k, (src, dst) in enumerate(((xa.at[0:2], xa_v), (dza, dza_v), (xb, xb_v), (dzb, dzb_v)))
     ]
+    smalls = [pltpu.make_async_copy(src, dst, small_sem.at[k]) for k, (src, dst) in enumerate(((vec, vec_ref), (x_ends, x_tails), (g_ends, g_tails)))]
     sides = [pltpu.make_async_copy(src, dst, side_sem.at[k]) for k, (src, dst) in enumerate(((z, z_v), (z_near, zn_v), (dx, dx_v)))]
     outs = [pltpu.make_async_copy(src, dst, out_sem.at[k]) for k, (src, dst) in enumerate(((z_st, z_out), (dx_st, dx_out)))]
 
@@ -462,9 +501,10 @@
 
     @pl.when((step == 0) & (stage == 1))
     def _():
-        for copy in fetches:
+        images = ((xa_v, dza_v, ga_ref, gsa_ref), (xb_v, dzb_v, gb_ref, gsb_ref))
+        for copy in [smalls[0]] + fetches[:2] + smalls[1:]:
             copy.start()
-        images = ((xa_v, dza_v, ga_ref, gsa_ref), (xb_v, dzb_v, gb_ref, gsb_ref))
+        smalls[0].wait()
         for k, (x_v, dz_v, g_ref, gs_ref) in enumerate(images):
             fetches[2 * k].wait()
             for q in range(2):
@@ -472,26 +512,34 @@
                 xt_ref[rows, k * MAIN:(k + 1) * MAIN] = x_v[q, :MAIN, :].T
             fetches[2 * k + 1].wait()
             if k == 0:
+                for copy in fetches[2:]:
+                    copy.start()
+            else:
                 sum_fetch(0).start()
                 sum_fetch(1).start()
             gs_ref[...] = (dz_v[...].astype(F32) * vec_ref[2:3, :]).astype(BF16)
-        sides[0].start()
-        sides[1].start()
-        sum_fetch(2).start()
-        sum_fetch(3).start()
+            if k == 0:
+                tot_v[0] = jnp.dot(xt_ref[:, :MAIN], gsa_ref[:MAIN], preferred_element_type=F32)
+        for copy in smalls[1:]:
+            copy.wait()
         for q in range(2):
             rows = slice(q * CHUNK, (q + 1) * CHUNK)
             ends = [xa_v[q, MAIN:, :], xb_v[q, MAIN:, :], x_tails[0, q], x_tails[1, q]]
             xt_ref[rows, 2 * MAIN:] = jnp.concatenate(ends, axis=0).T
-        sum_fetch(0).wait()
-        sum_fetch(1).wait()
-        total = product([gsa_ref[:MAIN], gsb_ref[:MAIN], gsa_ref[MAIN:], gsb_ref[MAIN:], g_tails[0, 9], g_tails[1, 9]])
+        rest = jnp.concatenate([gsb_ref[:MAIN], gsa_ref[MAIN:], gsb_ref[MAIN:], g_tails[0, 9], g_tails[1, 9]], axis=0)
+        total = jnp.dot(xt_ref[:, MAIN:], rest, preferred_element_type=F32)
         for x_v, dz_v, g_ref, gs_ref in images:
             for n in range(CH // TILE):
                 cols = slice(n * TILE, (n + 1) * TILE)
                 fill_halo(g_ref.at[:, :, cols], (dz_v[:, cols].astype(F32) * vec_ref[0:1, cols]).astype(BF16))
-        tot_v[0] = total + sum_v[0]
+        for copy in sides[:2]:
+            copy.start()
+        sum_fetch(2).start()
+        sum_fetch(3).start()
+        sum_fetch(0).wait()
+        tot_v[0] += total + sum_v[0]
         short_copy.start()
+        sum_fetch(1).wait()
         tot_v[1] = tap_product(0) + sum_v[1]
         tot_copy(1).start()
 
@@ -521,8 +569,7 @@
         for k in range(2):
             term = 2 * step + k
             tot_v[term % SLOTS] = tap_product(term - 1) + sum_v[term % SLOTS]
-        tot_copy(2 * step).start()
-        tot_copy(2 * step + 1).start()
+            tot_copy(term).start()
 
     @pl.when((step == 0) & (stage == 0))
     def _():
@@ -577,16 +624,13 @@
 
 
 def last(x_far, x_diag, x_tails, dzm_far, dzm_diag, vec, g_tails, sums, z, z_near, dx):
-    def whole(shape):
-        return pl.BlockSpec(shape, lambda s: (0,) * len(shape))
-
     anywhere = pl.BlockSpec(memory_space=pl.ANY)
     dma = pltpu.SemaphoreType.DMA
     z_shape, dx_shape = (SIDE, SIDE, 2, HALF), (1, 1, SIDE, SIDE, CH)
     dw, ds, z_out, dx_out = pl.pallas_call(
         last_kernel,
         grid=(5,),
-        in_specs=[anywhere, anywhere, whole((2, 2, GRP, CHUNK)), anywhere, anywhere, whole((3, CH)), whole((2, 10, GRP, CH))] + [anywhere] * 4,
+        in_specs=[anywhere] * 11,
         out_specs=[anywhere] * 4,
         out_shape=[
             jax.ShapeDtypeStruct((1, 3, 3, HALF, CH), F32),
@@ -599,6 +643,9 @@
             pltpu.VMEM((2, PIX, CHUNK), BF16),
             pltpu.VMEM((PIX, CH), BF16),
             pltpu.VMEM((PIX, CH), BF16),
+            pltpu.VMEM((2, 2, GRP, CHUNK), BF16),
+            pltpu.VMEM((3, CH), F32),
+            pltpu.VMEM((2, 10, GRP, CH), BF16),
             pltpu.VMEM((SLOTS, HALF, CH), F32),
             pltpu.VMEM((SLOTS, HALF, CH), F32),
             pltpu.VMEM((PIX, HALF), BF16),
@@ -611,7 +658,7 @@
             pltpu.VMEM((PIX, CH), BF16),
             pltpu.VMEM((PIX, CH), BF16),
             pltpu.VMEM((HALF, 2 * PIX + 2 * GRP), BF16),
-            dma((4,)), dma((SLOTS,)), dma((SLOTS,)), dma((3,)), dma((2,)),
+            dma((4,)), dma((3,)), dma((SLOTS,)), dma((SLOTS,)), dma((3,)), dma((2,)),
         ],
         compiler_params=params(1),
         cost_estimate=cost(2 * FWD_FLOPS, 2 * W_BYTES),

time: 117 us -> 112 us (0.957)
  Pallas kernels: 116 us -> 111 us
    pallas_call x1, Pallas kernels: 87.2 us -> 84 us  [main(): pl.pallas_call(main_kernel, in_specs=[anywhere] * 2 + [vmem] * 3 + [anywh...]
where the time goes in v5:
time: 112 us
  Pallas kernels  111 us (99%)
    pallas_call x1, Pallas kernels, main(): pl.pallas_call(main_kernel, in_specs=[anywhere] * 2 + [vmem] * 3 + [anywh...  84 us
    pallas_call x1, Pallas kernels, last(): pl.pallas_call(last_kernel, grid=(5,), in_specs=[anywhere] * 11, out_spec...  27.4 us

profile of v5, /device:TPU:2, one launch (start us, length us, event | category | flops | bytes accessed | tf_op | source)
XLA Modules:
  0.0 112.2 jit_solution(9270648432320209170)
XLA Ops:
  0.6 84.0 %main.1 = (bf16[4,784,256]{2,1,0:T(8,128)(2,1)}, bf16[2,784,256]{2,1,0:T(8,128)(2,1)}, bf16[2,2,16,256]{3,2,1,0:T(8,128)(2,1)}, bf16[9,512,1024]{2,1,0:T(8,128)(...) custom-call(bf16[1,1,28,28,1024]{4,3,2,1,0:T(8,128)(2,1)} %act.1, ...), custom_call_target="tpu_custom_call" | custom-call | flops 49325015040 | bytes 20971520 | tf_op jit(solution)/shard_map/main/pallas_call | solution.py:416
  84.6 27.4 %last.1 = (f32[1,3,3,512,1024]{4,3,2,1,0:T(8,128)}, f32[1,512,1024]{2,1,0:T(8,128)}, bf16[28,28,2,512]{3,2,1,0:T(2,128)(2,1)}, bf16[1,1,28,28,1024]{4,3,2,1,0:T(8,128)(2,1)}) custom-call(bf16[4,784,256]{2,1,0:T(8,128)(2,1)} %get-tuple-element.19.xa, bf16[2,784,256]{2,1,0:T(8,128)(2,1)} %get-tuple-element.20.xb, ...), custom_call_target="tpu_custom_call" | custom-call | flops 16441671680 | bytes 20971520 | tf_op jit(solution)/shard_map/last/pallas_call | solution.py:630

commit v6 on v5

--- a/solution.py
+++ b/solution.py
@@ -502,7 +502,7 @@
     @pl.when((step == 0) & (stage == 1))
     def _():
         images = ((xa_v, dza_v, ga_ref, gsa_ref), (xb_v, dzb_v, gb_ref, gsb_ref))
-        for copy in [smalls[0]] + fetches[:2] + smalls[1:]:
+        for copy in [smalls[0]] + fetches + smalls[1:]:
             copy.start()
         smalls[0].wait()
         for k, (x_v, dz_v, g_ref, gs_ref) in enumerate(images):
@@ -511,10 +511,7 @@
                 rows = slice(q * CHUNK, (q + 1) * CHUNK)
                 xt_ref[rows, k * MAIN:(k + 1) * MAIN] = x_v[q, :MAIN, :].T
             fetches[2 * k + 1].wait()
-            if k == 0:
-                for copy in fetches[2:]:
-                    copy.start()
-            else:
+            if k == 1:
                 sum_fetch(0).start()
                 sum_fetch(1).start()
             gs_ref[...] = (dz_v[...].astype(F32) * vec_ref[2:3, :]).astype(BF16)

time: 112 us -> 112 us (level)
  no operation moved by 1% of the time
where the time goes in v6:
time: 112 us
  Pallas kernels  111 us (99%)
    pallas_call x1, Pallas kernels, main(): pl.pallas_call(main_kernel, in_specs=[anywhere] * 2 + [vmem] * 3 + [anywh...  84 us
    pallas_call x1, Pallas kernels, last(): pl.pallas_call(last_kernel, grid=(5,), in_specs=[anywhere] * 11, out_spec...  26.9 us

profile of v6, /device:TPU:2, one launch (start us, length us, event | category | flops | bytes accessed | tf_op | source)
XLA Modules:
  0.0 111.6 jit_solution(10489820691986811088)
XLA Ops:
  0.6 84.0 %main.1 = (bf16[4,784,256]{2,1,0:T(8,128)(2,1)}, bf16[2,784,256]{2,1,0:T(8,128)(2,1)}, bf16[2,2,16,256]{3,2,1,0:T(8,128)(2,1)}, bf16[9,512,1024]{2,1,0:T(8,128)(...) custom-call(bf16[1,1,28,28,1024]{4,3,2,1,0:T(8,128)(2,1)} %act.1, ...), custom_call_target="tpu_custom_call" | custom-call | flops 49325015040 | bytes 20971520 | tf_op jit(solution)/shard_map/main/pallas_call | solution.py:416
  84.6 26.9 %last.1 = (f32[1,3,3,512,1024]{4,3,2,1,0:T(8,128)}, f32[1,512,1024]{2,1,0:T(8,128)}, bf16[28,28,2,512]{3,2,1,0:T(2,128)(2,1)}, bf16[1,1,28,28,1024]{4,3,2,1,0:T(8,128)(2,1)}) custom-call(bf16[4,784,256]{2,1,0:T(8,128)(2,1)} %get-tuple-element.19.xa, bf16[2,784,256]{2,1,0:T(8,128)(2,1)} %get-tuple-element.20.xb, ...), custom_call_target="tpu_custom_call" | custom-call | flops 16441671680 | bytes 20971520 | tf_op jit(solution)/shard_map/last/pallas_call | solution.py:627
